TPU v7x, 32 devices: a whole 2x2x4 slice. The times are simulated.
32 devices in a mesh: ep: 32 (over z, y, x, core).
Axes of the slice: x: 2, y: 2, z: 4, core: 2. Of those that a mesh axis runs over, the one named last changes fastest.
Arguments:
- x_tokens: bfloat16 [32768, 1024], P('ep')
- w_router: bfloat16 [1024, 32], replicated
- w_gate: bfloat16 [32, 1024, 512], P('ep')
- w_up: bfloat16 [32, 1024, 512], P('ep')
- w_down: bfloat16 [32, 512, 1024], P('ep')
- topk_idx: int32 [32768, 8], P('ep')
- dy_tokens: bfloat16 [32768, 1024], P('ep')
Outputs:
- output 1: bfloat16 [32768, 1024], P('ep')
- output 2: float32 [], replicated
- output 3: bfloat16 [32768, 1024], P('ep')
- output 4: float32 [1024, 32], replicated
- output 5: float32 [32, 1024, 512], P('ep')
- output 6: float32 [32, 1024, 512], P('ep')
- output 7: float32 [32, 512, 1024], P('ep')
All inputs are finite; a program needn't handle non-finite values.
Results may differ from a plain program's by a relative error of at most 0.00541992.
Values are sent between devices in bfloat16 or wider.
A program may use at most 1 GiB of HBM per device.

v0:
```python
import jax
import jax.numpy as jnp
from jax import lax
from jax.sharding import PartitionSpec as P

AUX_COEF = 0.001


def route_slots(idx_dev, n_exp, capacity):
    tok_count, top_k = idx_dev.shape
    choice_mask = idx_dev[:, :, None] == jnp.arange(n_exp, dtype=jnp.int32)
    expert_hot = jnp.sum(choice_mask.astype(jnp.int32), axis=1)
    earlier = jnp.cumsum(expert_hot, axis=0) - expert_hot
    position = jnp.take_along_axis(earlier, idx_dev, axis=1)
    slot_ids = jnp.where(position < capacity, idx_dev * capacity + position, n_exp * capacity)
    pair_ids = jnp.arange(tok_count * top_k, dtype=jnp.int32)
    empty_fill = jnp.full((n_exp * capacity,), tok_count * top_k, jnp.int32)
    pair_of_slot = empty_fill.at[slot_ids.reshape(-1)].set(pair_ids, mode="drop")
    return slot_ids, pair_of_slot, choice_mask, expert_hot


def solution(mesh):
    n_dev = mesh.shape["ep"]

    def local_block(x_loc, w_router, wg_loc, wu_loc, wd_loc, idx_loc, dy_loc):
        tok_count, model_dim = x_loc.shape
        top_k = idx_loc.shape[1]
        n_exp = w_router.shape[1]
        loc_exp = wg_loc.shape[0]
        capacity = (5 * tok_count * top_k + 4 * n_exp - 1) // (4 * n_exp)
        n_total = tok_count * n_dev
        logits = jnp.dot(x_loc, w_router, preferred_element_type=jnp.float32)
        router_prob = jax.nn.softmax(logits, axis=-1)
        pick_prob = jnp.take_along_axis(router_prob, idx_loc, axis=1)
        pick_sum = jnp.sum(pick_prob, axis=1, keepdims=True)
        gate_f32 = pick_prob / pick_sum
        gate_bf = gate_f32.astype(jnp.bfloat16)
        slot_ids, pair_of_slot, choice_mask, expert_hot = route_slots(idx_loc, n_exp, capacity)
        tok_of_slot = pair_of_slot // top_k
        buf_shape = (n_dev, loc_exp, capacity, model_dim)

        send_x = jnp.take(x_loc, tok_of_slot, axis=0, mode="fill", fill_value=0).reshape(buf_shape)
        recv_x = lax.all_to_all(send_x, "ep", 0, 1)
        gate_pre = jnp.einsum("egcd,edf->egcf", recv_x, wg_loc, preferred_element_type=jnp.float32)
        up_pre = jnp.einsum("egcd,edf->egcf", recv_x, wu_loc, preferred_element_type=jnp.float32)
        act_gate = jax.nn.silu(gate_pre)
        hidden = (act_gate * up_pre).astype(jnp.bfloat16)
        out_slot = jnp.einsum("egcf,efd->egcd", hidden, wd_loc, preferred_element_type=jnp.float32).astype(jnp.bfloat16)
        back_out = lax.all_to_all(out_slot, "ep", 1, 0).reshape(n_exp * capacity, model_dim)
        out_tok = jnp.take(back_out, slot_ids, axis=0, mode="fill", fill_value=0)
        y_loc = jnp.einsum("tk,tkd->td", gate_bf, out_tok, preferred_element_type=jnp.float32).astype(jnp.bfloat16)

        load_stats = jnp.concatenate([jnp.sum(expert_hot, axis=0).astype(jnp.float32), jnp.sum(router_prob, axis=0)])
        load_stats = lax.psum(load_stats, "ep")
        load_frac = load_stats[:n_exp] / (n_total * top_k)
        mean_prob = load_stats[n_exp:] / n_total
        aux_loss = AUX_COEF * n_exp * jnp.sum(load_frac * mean_prob)

        gate_slot = jnp.take(gate_bf.reshape(-1), pair_of_slot, mode="fill", fill_value=0)
        dy_slot = jnp.take(dy_loc, tok_of_slot, axis=0, mode="fill", fill_value=0)
        send_do = (gate_slot[:, None] * dy_slot).reshape(buf_shape)
        recv_do = lax.all_to_all(send_do, "ep", 0, 1)
        dw_down = jnp.einsum("egcf,egcd->efd", hidden, recv_do, preferred_element_type=jnp.float32)
        d_hidden = jnp.einsum("egcd,efd->egcf", recv_do, wd_loc, preferred_element_type=jnp.float32).astype(jnp.bfloat16).astype(jnp.float32)
        sigmoid_g = jax.nn.sigmoid(gate_pre)
        d_gate_pre = (d_hidden * up_pre * sigmoid_g * (1.0 + gate_pre * (1.0 - sigmoid_g))).astype(jnp.bfloat16)
        d_up_pre = (d_hidden * act_gate).astype(jnp.bfloat16)
        dw_gate = jnp.einsum("egcd,egcf->edf", recv_x, d_gate_pre, preferred_element_type=jnp.float32)
        dw_up = jnp.einsum("egcd,egcf->edf", recv_x, d_up_pre, preferred_element_type=jnp.float32)
        dx_slot = (jnp.einsum("egcf,edf->egcd", d_gate_pre, wg_loc, preferred_element_type=jnp.float32)
                   + jnp.einsum("egcf,edf->egcd", d_up_pre, wu_loc, preferred_element_type=jnp.float32)).astype(jnp.bfloat16)
        back_dx = lax.all_to_all(dx_slot, "ep", 1, 0).reshape(n_exp * capacity, model_dim)
        dx_tok = jnp.take(back_dx, slot_ids, axis=0, mode="fill", fill_value=0)
        dx_expert = jnp.sum(dx_tok, axis=1, dtype=jnp.float32)

        d_gate = jnp.einsum("tkd,td->tk", out_tok, dy_loc, preferred_element_type=jnp.float32)
        d_pick = (d_gate - jnp.sum(d_gate * gate_f32, axis=1, keepdims=True)) / pick_sum
        d_prob = jnp.sum(jnp.where(choice_mask, d_pick[:, :, None], 0.0), axis=1) + AUX_COEF * n_exp * load_frac / n_total
        d_logit = router_prob * (d_prob - jnp.sum(router_prob * d_prob, axis=1, keepdims=True))
        d_logit_bf = d_logit.astype(jnp.bfloat16)
        dw_router = lax.psum(jnp.einsum("td,te->de", x_loc, d_logit_bf, preferred_element_type=jnp.float32), "ep")
        dx_loc = (dx_expert + jnp.einsum("te,de->td", d_logit_bf, w_router, preferred_element_type=jnp.float32)).astype(jnp.bfloat16)
        return y_loc, aux_loss, dx_loc, dw_router, dw_gate, dw_up, dw_down

    tok_spec = P("ep")
    return jax.shard_map(
        local_block,
        mesh=mesh,
        in_specs=(tok_spec, P(), tok_spec, tok_spec, tok_spec, tok_spec, tok_spec),
        out_specs=(tok_spec, P(), tok_spec, P(), tok_spec, tok_spec, tok_spec),
        check_vma=False,
    )
```

profile of v0, /device:TPU:0, one launch (start us, length us, event | category | flops | bytes accessed | tf_op | source)
XLA Modules:
  0.0 2588.2 jit_solution(16462048653701564438)
XLA Ops:
  7.2 0.9 bitcast_or_fusion
  8.1 1.5 convert_reduce_fusion.1
  9.7 9.0 reduce-window.6
  19.6 65.5 %gather_fusion.2 = s32[8192]{0:T(1024)S(1)} fusion(s32[1024,32]{0,1:T(8,128)S(1)} %fusion.42, s32[8192]{0:T(1024)S(1)} %reshape.237), kind=kCustom, calls=%fused_computation.6 | custom fusion | bytes 131072 | tf_op jit(solution)/shard_map/jit(take_along_axis)/gather | solution.py:14
  85.2 0.3 reshape.246
  85.7 0.6 compare_and_fusion.1
  86.5 0.3 reshape.191
  86.9 30.5 %scatter_custom_fusion = s32[10240]{0:T(1024)S(1)} fusion(s32[8192]{0:T(1024)S(1)} %bitcast.131, s32[8192]{0:T(1024)S(1)} %iota.7, s32[]{:T(128)} %constant.76.clone.1), kind=kCustom, calls=%fused_computation.92 | custom fusion | bytes 40964 | tf_op jit(solution)/shard_map/scatter | solution.py:18
  117.3 0.6 compare_and_fusion
  118.0 0.7 fusion.47
  118.7 2.3 fusion.58
  121.0 0.6 fusion.56
  121.7 65.5 %gather_fusion.1 = f32[8192]{0:T(1024)S(1)} fusion(f32[1024,32]{0,1:T(8,128)S(1)} %get-tuple-element.12, s32[8192]{0:T(1024)S(1)} %reshape.237), kind=kCustom, calls=%fused_computation.5 | custom fusion | bytes 131072 | tf_op jit(solution)/shard_map/jit(take_along_axis)/gather | solution.py:34
  187.8 0.6 copy-done.8
  188.4 0.6 copy-done.20
  189.4 63.3 %gather_fusion = bf16[10240]{0:T(1024)(128)(2,1)S(1)} fusion(bf16[8192]{0:T(1024)(128)(2,1)S(1)} %convert_element_type.59, s32[10240]{0:T(1024)S(1)} %copy-done.15), kind=kCustom, calls=%fused_computation.4 | custom fusion | bytes 81920 | tf_op jit(solution)/shard_map/jit(_take)/gather | solution.py:59
  252.7 52.2 %gather_fusion.3 = bf16[10240,1024]{1,0:T(8,128)(2,1)} fusion(bf16[1024,1024]{1,0:T(8,128)(2,1)} %param.11, s32[10240]{0:T(1024)S(1)} %copy-done.10), kind=kCustom, calls=%fused_computation.clone | custom fusion | bytes 41984000 | tf_op jit(solution)/shard_map/jit(_take)/gather | solution.py:42
  304.9 43.9 %gather_fusion.5 = bf16[10240,1024]{1,0:T(8,128)(2,1)} fusion(bf16[1024,1024]{1,0:T(8,128)(2,1)S(1)} %copy-done, s32[10240]{0:T(1024)S(1)} %copy-done.10), kind=kCustom, calls=%fused_computation.2.clone | custom fusion | bytes 41984000 | tf_op jit(solution)/shard_map/jit(_take)/gather | solution.py:60
  348.8 28.2 %select_multiply_fusion = (bf16[10240,1024]{1,0:T(8,128)(2,1)}, bf16[10240,1024]{1,0:T(8,128)(2,1)}) fusion(bf16[10240,1024]{1,0:T(8,128)(2,1)} %gather_fusion.5, pred[10240]{0:T(1024)(128)(4,1)S(1)} %copy-done.22, bf16[10240]{0:T(1024)(128)(2,1)S(1)} %and_select_fusion, bf16[10240,1024]{1,0:T(8,128)(2,1)} %gather_fusion.3), kind=kLoop, calls=%fused_computation.29 | loop fusion | flops 31457280 | bytes 83916800 | tf_op jit(solution)/shard_map/mul | solution.py:61
  377.0 468.8 %all_to_all.16 = bf16[32,1,1,320,1024]{4,3,2,1,0:T(8,128)(2,1)} all-to-all(bf16[32,1,1,320,1024]{4,3,2,1,0:T(8,128)(2,1)} %bitcast.125), channel_id=1, replica_groups=mesh['ep'=32] {'ep'}, dimensions={0} | all-to-all | bytes 41943040 | tf_op jit(solution)/shard_map/all_to_all | solution.py:62
  845.8 7.5 all-to-all-start
  853.3 20.8 fusion.22
  874.1 412.4 %all-to-all-done = bf16[32,1,1,320,1024]{4,3,2,1,0:T(8,128)(2,1)} async-done(((bf16[32,1,1,320,1024]{4,3,2,1,0:T(8,128)(2,1)}), bf16[32,1,1,320,1024]{4,3,2,1,0:T(8,128)(2,1)}, u32[]{:S(2)}, u32[]{:S(2)}) %all-to-all-start) | async-done | bytes 20971552 | tf_op jit(solution)/shard_map/all_to_all | solution.py:43
  1286.5 19.4 fusion.15
  1305.9 34.7 %fusion.2 = (bf16[32,320,512]{2,1,0:T(8,128)(2,1)}, bf16[32,320,512]{2,1,0:T(8,128)(2,1)}, bf16[32,320,512]{2,1,0:T(8,128)(2,1)}) fusion(bf16[32,320,512]{2,1,0:T(8,128)(2,1)} %fusion.22, f32[32,320,512]{2,1,0:T(8,128)} %fusion.15, bf16[1,1024,512]{2,1,0:T(8,128)(2,1)S(1)} %copy-done.28, bf16[32,1,1,320,1024]{4,3,2,1,0:T(8,128)(2,1)} %all-to-all-done), kind=kOutput, calls=%fused_computation.14 | convolution fusion | flops 10821304320 | bytes 84934656 | tf_op jit(solution)/shard_map/egcd,edf->egcf/dot_general | solution.py:45
  1340.6 18.1 convert_bitcast_fusion
  1358.7 30.3 %all-to-all-start.1 = ((bf16[1,1,32,320,1024]{4,3,1,0,2:T(8,128)(2,1)}), bf16[1,1,32,320,1024]{4,3,1,0,2:T(8,128)(2,1)}, u32[]{:S(2)}, u32[]{:S(2)}) async-start(bf16[1,1,32,320,1024]{4,3,1,0,2:T(8,128)(2,1)} %convert_bitcast_fusion), calls=%async_computation.1 | async-start | bytes 41943040 | tf_op jit(solution)/shard_map/all_to_all | solution.py:49
  1389.0 21.2 fusion.39
  1410.2 25.5 fusion.4
  1435.7 386.4 %all-to-all-done.1 = bf16[1,1,32,320,1024]{4,3,1,0,2:T(8,128)(2,1)} async-done(((bf16[1,1,32,320,1024]{4,3,1,0,2:T(8,128)(2,1)}), bf16[1,1,32,320,1024]{4,3,1,0,2:T(8,128)(2,1)}, u32[]{:S(2)}, u32[]{:S(2)}) %all-to-all-start.1) | async-done | bytes 20971552 | tf_op jit(solution)/shard_map/all_to_all | solution.py:49
  1822.1 28.3 %all-to-all-start.3 = ((bf16[1,1,32,320,1024]{4,3,1,0,2:T(8,128)(2,1)}), bf16[1,1,32,320,1024]{4,3,1,0,2:T(8,128)(2,1)}, u32[]{:S(2)}, u32[]{:S(2)}) async-start(bf16[1,1,32,320,1024]{4,3,1,0,2:T(8,128)(2,1)} %fusion.4), calls=%async_computation.3 | async-start | bytes 41943040 | tf_op jit(solution)/shard_map/all_to_all | solution.py:72
  1851.2 0.4 copy.71
  1851.7 476.0 %psum.14 = f32[64]{0:T(128)S(1)} all-reduce(f32[64]{0:T(128)S(1)} %pad_maximum_fusion), channel_id=1, replica_groups=mesh['ep'=32] {'ep'}, use_global_device_ids=true, to_apply=%region_9.12 | all-reduce | flops 64 | bytes 512 | tf_op jit(solution)/shard_map/psum | solution.py:54
  2327.7 0.7 slice_multiply_fusion
  2329.1 18.3 fusion.26
  2347.3 18.2 fusion.29
  2365.6 16.3 fusion.32
  2381.9 50.2 %gather_fusion.4 = bf16[8192,1024]{1,0:T(8,128)(2,1)} fusion(bf16[10240,1024]{1,0:T(8,128)(2,1)} %bitcast.17, s32[8192]{0:T(1024)S(1)} %broadcast_clamp_fusion.1), kind=kCustom, calls=%fused_computation.1.clone | custom fusion | bytes 33587200 | tf_op jit(solution)/shard_map/jit(_take)/gather | solution.py:50
  2432.1 14.3 fusion.18
  2446.4 1.1 copy.74
  2447.9 2.7 convolution_bitcast_fusion
  2450.7 10.9 fusion.19
  2461.5 50.2 %gather_fusion.6 = bf16[8192,1024]{1,0:T(8,128)(2,1)} fusion(bf16[10240,1024]{1,0:T(8,128)(2,1)} %bitcast.25, s32[8192]{0:T(1024)S(1)} %broadcast_clamp_fusion.1), kind=kCustom, calls=%fused_computation.3.clone | custom fusion | bytes 33587200 | tf_op jit(solution)/shard_map/jit(_take)/gather | solution.py:73
  2511.7 14.0 convert_reduce_fusion
  2525.7 2.1 add_convert_fusion.1
  2527.8 2.1 copy.81
  2529.9 48.5 %all-reduce.2.cloned.1.call-done = f32[1024,32]{0,1:T(8,128)} async-done(((f32[1024,32]{0,1:T(8,128)}), f32[1024,32]{0,1:T(8,128)}) %all-reduce.2.cloned.1.call-update) | async-done | bytes 131088 | tf_op jit(solution)/shard_map/psum | solution.py:81
  2578.4 1.6 copy.83
  (100 shorter events, 3.6 us)
Async XLA Ops:
  7.2 297.8 %copy-start = (bf16[1024,1024]{1,0:T(8,128)(2,1)S(1)}, bf16[1024,1024]{1,0:T(8,128)(2,1)}, u32[]{:S(2)}) copy-start(bf16[1024,1024]{1,0:T(8,128)(2,1)} %param.17) | copy-start | bytes 6291460
  19.6 66.0 %copy-start.6 = (s32[1024,8]{0,1:T(8,128)S(1)}, s32[1024,8]{0,1:T(8,128)}, u32[]{:S(2)}) copy-start(s32[1024,8]{0,1:T(8,128)} %param.16) | copy-start | bytes 98308
  19.6 99.0 %copy-start.13 = (bf16[1024,32]{0,1:T(8,128)(2,1)S(1)}, bf16[1024,32]{0,1:T(8,128)(2,1)}, u32[]{:S(2)}) copy-start(bf16[1024,32]{0,1:T(8,128)(2,1)} %param.12) | copy-start | bytes 196612
  86.3 35.4 %copy-start.11 = (s32[1024,8]{0,1:T(8,128)}, s32[1024,8]{0,1:T(8,128)S(1)}, u32[]{:S(2)}) copy-start(s32[1024,8]{0,1:T(8,128)S(1)} %get-tuple-element.14) | copy-start | bytes 98308
  117.3 3.7 copy-start.4
  121.7 65.6 %copy-start.1 = (f32[1024,32]{0,1:T(8,128)}, f32[1024,32]{0,1:T(8,128)S(1)}, u32[]{:S(2)}) copy-start(f32[1024,32]{0,1:T(8,128)S(1)} %get-tuple-element.12) | copy-start | bytes 393220
  121.7 66.1 %copy-start.18 = (pred[1024,8]{0,1:T(8,128)(4,1)S(1)}, pred[1024,8]{0,1:T(8,128)(4,1)}, u32[]{:S(2)}) copy-start(pred[1024,8]{0,1:T(8,128)(4,1)} %get-tuple-element.15) | copy-start | bytes 24580
  121.7 67.7 %copy-start.15 = (s32[10240]{0:T(1024)S(1)}, s32[10240]{0:T(1024)}, u32[]{:S(2)}) copy-start(s32[10240]{0:T(1024)} %get-tuple-element.19) | copy-start | bytes 122884
  187.2 65.4 %copy-start.5 = (s32[10240]{0:T(1024)S(1)}, s32[10240]{0:T(1024)}, u32[]{:S(2)}) copy-start(s32[10240]{0:T(1024)} %copy-done.4) | copy-start | bytes 122884
  187.2 65.5 %copy-start.10 = (s32[10240]{0:T(1024)S(1)}, s32[10240]{0:T(1024)}, u32[]{:S(2)}) copy-start(s32[10240]{0:T(1024)} %get-tuple-element.20) | copy-start | bytes 122884
  187.7 0.6 copy-start.8
  188.4 0.6 copy-start.20
  189.0 116.0 %copy-start.16 = (bf16[1024,8]{0,1:T(8,128)(2,1)}, bf16[1024,8]{0,1:T(8,128)(2,1)S(1)}, u32[]{:S(2)}) copy-start(bf16[1024,8]{0,1:T(8,128)(2,1)S(1)} %fusion.53) | copy-start | bytes 49156
  304.9 43.9 %copy-start.22 = (pred[10240]{0:T(1024)(128)(4,1)S(1)}, pred[10240]{0:T(1024)(128)(4,1)}, u32[]{:S(2)}) copy-start(pred[10240]{0:T(1024)(128)(4,1)} %compare_and_fusion) | copy-start | bytes 30724
  845.8 7.5 copy-start.26
  845.8 440.6 %all-to-all-start = ((bf16[32,1,1,320,1024]{4,3,2,1,0:T(8,128)(2,1)}), bf16[32,1,1,320,1024]{4,3,2,1,0:T(8,128)(2,1)}, u32[]{:S(2)}, u32[]{:S(2)}) async-start(bf16[32,1,1,320,1024]{4,3,2,1,0:T(8,128)(2,1)} %bitcast.124), calls=%async_computation | async-start | bytes 41943040 | tf_op jit(solution)/shard_map/all_to_all | solution.py:43
  1286.5 19.4 copy-start.28
  1358.7 30.3 %copy-start.27 = (bf16[1,1024,512]{2,1,0:T(8,128)(2,1)S(1)}, bf16[1,1024,512]{2,1,0:T(8,128)(2,1)}, u32[]{:S(2)}) copy-start(bf16[1,1024,512]{2,1,0:T(8,128)(2,1)} %param.13) | copy-start | bytes 3145732
  1358.7 463.4 %all-to-all-start.1 = ((bf16[1,1,32,320,1024]{4,3,1,0,2:T(8,128)(2,1)}), bf16[1,1,32,320,1024]{4,3,1,0,2:T(8,128)(2,1)}, u32[]{:S(2)}, u32[]{:S(2)}) async-start(bf16[1,1,32,320,1024]{4,3,1,0,2:T(8,128)(2,1)} %convert_bitcast_fusion), calls=%async_computation.1 | async-start | bytes 41943040 | tf_op jit(solution)/shard_map/all_to_all | solution.py:49
  1435.7 414.8 %copy-start.24 = (s32[32]{0:T(128)S(1)}, s32[32]{0:T(128)}, u32[]{:S(2)}) copy-start(s32[32]{0:T(128)} %get-tuple-element.9) | copy-start | bytes 388
  1435.7 414.8 %copy-start.23 = (pred[1024,8]{0,1:T(8,128)(4,1)S(1)}, pred[1024,8]{0,1:T(8,128)(4,1)}, u32[]{:S(2)}) copy-start(pred[1024,8]{0,1:T(8,128)(4,1)} %get-tuple-element.13) | copy-start | bytes 24580
  1435.7 415.0 %copy-start.12 = (s32[1024,8]{0,1:T(8,128)S(1)}, s32[1024,8]{0,1:T(8,128)}, u32[]{:S(2)}) copy-start(s32[1024,8]{0,1:T(8,128)} %copy-done.11) | copy-start | bytes 98308
  1435.7 415.5 %copy-start.17 = (bf16[1024,8]{0,1:T(8,128)(2,1)S(1)}, bf16[1024,8]{0,1:T(8,128)(2,1)}, u32[]{:S(2)}) copy-start(bf16[1024,8]{0,1:T(8,128)(2,1)} %copy-done.16) | copy-start | bytes 49156
  1435.7 415.9 %copy-start.25 = (f32[32]{0:T(128)S(1)}, f32[32]{0:T(128)}, u32[]{:S(2)}) copy-start(f32[32]{0:T(128)} %get-tuple-element.11) | copy-start | bytes 388
  1822.1 639.4 %all-to-all-start.3 = ((bf16[1,1,32,320,1024]{4,3,1,0,2:T(8,128)(2,1)}), bf16[1,1,32,320,1024]{4,3,1,0,2:T(8,128)(2,1)}, u32[]{:S(2)}, u32[]{:S(2)}) async-start(bf16[1,1,32,320,1024]{4,3,1,0,2:T(8,128)(2,1)} %fusion.4), calls=%async_computation.3 | async-start | bytes 41943040 | tf_op jit(solution)/shard_map/all_to_all | solution.py:72
  1850.4 728.0 %all-reduce.2.cloned.1.call-start = ((), (), s32[]{:S(2)}) async-start(), calls=%async_computation.4 | async-start | bytes 262144 | tf_op jit(solution)/shard_map/psum | solution.py:81
  2329.0 36.5 %slice-start = ((s8[10485760]{0:T(1024)(128)(4,1)}), s8[4194304]{0:T(1024)(128)(4,1)S(1)}, s32[]{:S(2)}) async-start(s8[10485760]{0:T(1024)(128)(4,1)} %bitcast.133), calls=%async_computation.5 | async-start | bytes 8388608
  2329.1 36.5 %slice-start.1 = ((s8[10485760]{0:T(1024)(128)(4,1)}), s8[4194304]{0:T(1024)(128)(4,1)S(1)}, s32[]{:S(2)}) async-start(s8[10485760]{0:T(1024)(128)(4,1)} %bitcast.133), calls=%async_computation.6 | async-start | bytes 8388608
  2347.3 18.2 slice-start.2
  2432.1 15.4 copy-start.9
  2432.1 15.4 copy-start.19
  2432.1 15.4 copy-start.21
  2432.1 15.5 copy-start.7
  2432.1 15.6 copy-start.2
  2511.7 14.0 copy-start.14
  2511.7 16.1 copy-start.3
Sparse Core Ops, SparseCore 0:
  2450.8 127.6 all-reduce.1
where the time goes:
time: 2590 us
  blocking collectives  945 us (36%)
  waiting for transfers between devices  847 us (33%)
  local copies, waits for them, and re-layouts  431 us (17%)
  matrix products  225 us (9%)
  starting transfers between devices  66.1 us (3%)
  other arithmetic  57.6 us (2%)
    psum x1, blocking collectives, local_block(): load_stats = lax.psum(load_stats, 'ep')  476 us
    all_to_all x1, blocking collectives, local_block(): recv_do = lax.all_to_all(send_do, 'ep', 0, 1)  469 us
    all_to_all x1, waiting for transfers between devices, local_block(): recv_x = lax.all_to_all(send_x, 'ep', 0, 1)  412 us
    all_to_all x1, waiting for transfers between devices, local_block(): lax.all_to_all(out_slot, 'ep', 1, 0).reshape(n_exp * capacity, model_dim)  386 us
    gather x5, local copies, waits for them, and re-layouts, local_block(): pick_prob = jnp.take_along_axis(router_prob, idx_loc, axis=1)  66.4 us
    gather x3, local copies, waits for them, and re-layouts, route_slots(): position = jnp.take_along_axis(earlier, idx_dev, axis=1)  66 us
    gather x1, local copies, waits for them, and re-layouts, local_block(): jnp.take(gate_bf.reshape(-1), pair_of_slot, mode='fill', fill_value=0)  63.3 us
    gather x1, local copies, waits for them, and re-layouts, local_block(): jnp.take(x_loc, tok_of_slot, axis=0, mode='fill', fill_value=0)  52.2 us
  transfers between devices with their start and end apart: 4, of which 3 were waited for; matrix products, arithmetic and copies ran while one was open for 10% of the time, Pallas kernels for 0%

commit v1 on v0

v1 whole, which is shorter than its diff:
```python
import functools

import jax
import jax.numpy as jnp
from jax import lax
from jax.experimental import pallas as pl
from jax.experimental.pallas import tpu as pltpu
from jax.sharding import PartitionSpec as P


AUX_COEF = 0.001
RING = (0, 1, 3, 2)
F32 = jnp.float32
BF16 = jnp.bfloat16


def device_perm(move):
    pairs = []
    for dev in range(32):
        z, y, x, core = move(dev // 8, (dev // 4) % 2, (dev // 2) % 2, dev % 2)
        pairs.append((dev, z * 8 + y * 4 + x * 2 + core))
    return pairs


RING_NEXT = {RING[i]: RING[(i + 1) % 4] for i in range(4)}
PERM_Z = device_perm(lambda z, y, x, c: (RING_NEXT[z], y, x, c))
PERM_X = device_perm(lambda z, y, x, c: (z, y, 1 - x, c))
PERM_Y = device_perm(lambda z, y, x, c: (z, 1 - y, x, c))
PERM_D = device_perm(lambda z, y, x, c: (z, 1 - y, 1 - x, c))
PERM_C = device_perm(lambda z, y, x, c: (z, y, x, 1 - c))


def send(value, perm):
    return lax.ppermute(value, "ep", perm)


def dot_nt(lhs, rhs):
    return lax.dot_general(lhs, rhs, (((1,), (1,)), ((), ())), preferred_element_type=F32)


def dot_tn(lhs, rhs):
    return lax.dot_general(lhs, rhs, (((0,), (0,)), ((), ())), preferred_element_type=F32)


def dot_nn(lhs, rhs):
    return jnp.dot(lhs, rhs, preferred_element_type=F32)


def params(limit_mib=60, **kwargs):
    return pltpu.CompilerParams(vmem_limit_bytes=limit_mib * 1024 * 1024, **kwargs)


def chosen_mask(idx_ref, n_exp, tok_count):
    expert_iota = lax.broadcasted_iota(jnp.int32, (n_exp, tok_count), 0)
    hot = jnp.zeros((n_exp, tok_count), F32)
    for k in range(idx_ref.shape[0]):
        hot = hot + jnp.where(expert_iota == idx_ref[k:k + 1, :], 1.0, 0.0)
    return hot


def route_kernel(capacity, x_ref, wr_ref, idx_ref, prob_ref, meta_ref, stat_ref):
    n_exp, tok_count = prob_ref.shape
    logits = lax.dot_general(wr_ref[...], x_ref[...], (((0,), (1,)), ((), ())), preferred_element_type=F32)
    expo = jnp.exp(logits - jnp.max(logits, axis=0, keepdims=True))
    prob = expo / jnp.sum(expo, axis=0, keepdims=True)
    prob_ref[...] = prob
    hot = chosen_mask(idx_ref, n_exp, tok_count)
    pick = hot * prob
    gate = pick / jnp.sum(pick, axis=0, keepdims=True)
    hot_bf = hot.astype(BF16)
    row = lax.broadcasted_iota(jnp.int32, (tok_count, 256), 0)
    lane = lax.broadcasted_iota(jnp.int32, (tok_count, 256), 1)
    for block in range(tok_count // 256):
        span = slice(block * 256, (block + 1) * 256)
        before = jnp.where(row < lane + block * 256, 1.0, 0.0).astype(BF16)
        earlier = dot_nn(hot_bf, before)
        keep = (hot[:, span] > 0.5) & (earlier < capacity)
        meta_ref[0:n_exp, span] = jnp.where(keep, earlier, -1.0)
    meta_ref[n_exp:2 * n_exp, :] = gate.astype(BF16).astype(F32)
    count = jnp.sum(hot, axis=1, keepdims=True)
    total = jnp.sum(prob, axis=1, keepdims=True)
    lanes = lax.broadcasted_iota(jnp.int32, (n_exp, tok_count), 1)
    stat_ref[...] = jnp.where(lanes < tok_count // 2, count, total)


def gather_kernel(capacity, eid_ref, x_ref, dy_ref, meta_ref, xs_ref, dr_ref, ws_ref, pos_ref, gate_ref):
    step = pl.program_id(0)
    n_exp = meta_ref.shape[0] // 2
    tok_count = x_ref.shape[0]
    slot = lax.broadcasted_iota(jnp.int32, (capacity, tok_count), 0).astype(F32)
    picks = []
    for b in range(2):
        j = step * 2 + b
        expert = eid_ref[j]
        pos = meta_ref[pl.ds(expert, 1), :]
        gate = meta_ref[pl.ds(expert + n_exp, 1), :]
        pos_ref[pl.ds(j, 1), :] = pos
        gate_ref[pl.ds(j, 1), :] = gate
        match = slot == pos
        weight = jnp.sum(jnp.where(match, gate, 0.0), axis=1, keepdims=True)
        ws_ref[b * capacity:(b + 1) * capacity, :] = jnp.broadcast_to(weight, (capacity, 128))
        picks.append(jnp.where(match, 1.0, 0.0).astype(BF16))
    pick = jnp.concatenate(picks, axis=0)
    xs_ref[...] = dot_nn(pick, x_ref[...]).astype(BF16)
    dr_ref[...] = dot_nn(pick, dy_ref[...]).astype(BF16)


def expert_kernel(slot_j, capacity, *refs):
    n_blk = 4
    xs, dr, ws, pos = refs[0:4], refs[4:8], refs[8:12], refs[12:16]
    wg, wu, wd = refs[16:19]
    o_out, dx_out, a_out, dwg_out, dwu_out, dwd_out = refs[19:25]
    (xs_v, dr_v, ws_v, pos_v, wg_v, wu_v, wd_v, o_v, dx_v, d_v, h_v, dg_v, du_v,
     dwg_v, dwu_v, dwd_v, in_sem, w_sem, out_sem, dw_sem) = refs[25:]
    tok_count = pos_v.shape[1]

    def weight_copies():
        pairs = ((wg, wg_v), (wu, wu_v), (wd, wd_v))
        return [pltpu.make_async_copy(src, dst, w_sem.at[i]) for i, (src, dst) in enumerate(pairs)]

    def row_copies(t, src_t):
        src = pl.ds(slot_j * capacity, capacity)
        dst = pl.ds(t * capacity, capacity)
        return [
            pltpu.make_async_copy(xs[src_t].at[src], xs_v.at[dst], in_sem.at[t, 0]),
            pltpu.make_async_copy(dr[src_t].at[src], dr_v.at[dst], in_sem.at[t, 1]),
            pltpu.make_async_copy(ws[src_t].at[src], ws_v.at[dst], in_sem.at[t, 2]),
        ]

    def out_copies(t):
        src = pl.ds(t * capacity, capacity)
        return [
            pltpu.make_async_copy(o_v.at[src], o_out.at[t], out_sem.at[t, 0]),
            pltpu.make_async_copy(dx_v.at[src], dx_out.at[t], out_sem.at[t, 1]),
        ]

    def dw_copies():
        pairs = ((dwg_v, dwg_out), (dwu_v, dwu_out), (dwd_v, dwd_out))
        return [pltpu.make_async_copy(src, dst, dw_sem.at[i]) for i, (src, dst) in enumerate(pairs)]

    for copy in weight_copies()[:2]:
        copy.start()
    for t in range(n_blk):
        for copy in row_copies(t, t):
            copy.start()
        if t == 0:
            weight_copies()[2].start()
    for t in range(n_blk):
        pos_v[t:t + 1, :] = pos[t][slot_j:slot_j + 1, :]
    slot = lax.broadcasted_iota(jnp.int32, (capacity, tok_count), 0).astype(F32)
    for copy in weight_copies():
        copy.wait()

    def block_body(t, carry):
        for copy in row_copies(t, 0):
            copy.wait()
        rows = pl.ds(pl.multiple_of(t * capacity, 64), capacity)
        x = xs_v[rows, :]
        g = dot_nn(x, wg_v[...])
        u = dot_nn(x, wu_v[...])
        sig = jax.nn.sigmoid(g)
        act = g * sig
        h = (act * u).astype(BF16)
        h_v[rows, :] = h
        o = dot_nn(h, wd_v[...]).astype(BF16)
        o_v[rows, :] = o
        d_raw = dr_v[rows, :].astype(F32)
        a = jnp.sum(o.astype(F32) * d_raw, axis=1, keepdims=True)
        a_out[pl.ds(t, 1), :] = jnp.sum(jnp.where(slot == pos_v[pl.ds(t, 1), :], a, 0.0), axis=0, keepdims=True)
        d = (ws_v[rows, 0:1] * d_raw).astype(BF16)
        d_v[rows, :] = d
        dh = dot_nt(d, wd_v[...]).astype(BF16).astype(F32)
        dg = (dh * u * sig * (1.0 + g * (1.0 - sig))).astype(BF16)
        du = (dh * act).astype(BF16)
        dg_v[rows, :] = dg
        du_v[rows, :] = du
        dx_v[rows, :] = (dot_nt(dg, wg_v[...]) + dot_nt(du, wu_v[...])).astype(BF16)
        for copy in out_copies(t):
            copy.start()
        return carry

    lax.fori_loop(0, n_blk, block_body, 0)

    def gate_body(m, carry):
        cols = pl.ds(pl.multiple_of(m * 256, 256), 256)
        x = xs_v[:, cols]
        dwg_v[cols, :] = dot_tn(x, dg_v[...])
        dwu_v[cols, :] = dot_tn(x, du_v[...])
        return carry

    lax.fori_loop(0, xs_v.shape[1] // 256, gate_body, 0)
    for copy in dw_copies()[:2]:
        copy.start()

    def down_body(m, carry):
        cols = pl.ds(pl.multiple_of(m * 256, 256), 256)
        dwd_v[cols, :] = dot_tn(h_v[:, cols], d_v[...])
        return carry

    lax.fori_loop(0, h_v.shape[1] // 256, down_body, 0)
    dw_copies()[2].start()
    for t in range(n_blk):
        for copy in out_copies(t):
            copy.wait()
    for copy in dw_copies():
        copy.wait()


def combine_kernel(capacity, *refs):
    o_refs, dx_refs = refs[0:8], refs[8:16]
    pos_ref, gate_ref, y_ref, dxo_ref = refs[16:]
    rows = y_ref.shape[0]
    start = pl.multiple_of(pl.program_id(0) * rows, rows)
    pos = pos_ref[:, pl.ds(start, rows)].T
    gate = gate_ref[:, pl.ds(start, rows)].T
    lane = lax.broadcasted_iota(jnp.int32, (rows, 2 * capacity), 1).astype(F32)
    first = lane < capacity
    y_acc = jnp.zeros(y_ref.shape, F32)
    dx_acc = jnp.zeros(y_ref.shape, F32)
    for k in range(4):
        pos_a, pos_b = pos[:, 2 * k:2 * k + 1], pos[:, 2 * k + 1:2 * k + 2]
        pos_b = jnp.where(pos_b < 0.0, -1.0, pos_b + capacity)
        match = lane == jnp.where(first, pos_a, pos_b)
        weight = jnp.where(first, gate[:, 2 * k:2 * k + 1], gate[:, 2 * k + 1:2 * k + 2])
        pick_w = jnp.where(match, weight, 0.0).astype(BF16)
        pick_1 = jnp.where(match, 1.0, 0.0).astype(BF16)
        o_pair = jnp.concatenate([o_refs[2 * k][0], o_refs[2 * k + 1][0]], axis=0)
        dx_pair = jnp.concatenate([dx_refs[2 * k][0], dx_refs[2 * k + 1][0]], axis=0)
        y_acc = y_acc + dot_nn(pick_w, o_pair)
        dx_acc = dx_acc + dot_nn(pick_1, dx_pair)
    y_ref[...] = y_acc
    dxo_ref[...] = dx_acc


def router_kernel(aux_scale, eid_ref, a0, a1, a2, a3, prob_ref, idx_ref, frac_ref, wr_ref, x_ref, dwr_ref, dxr_ref, a_v):
    n_exp, tok_count = prob_ref.shape
    for q, a_ref in enumerate((a0, a1, a2, a3)):
        for j in range(8):
            a_v[pl.ds(eid_ref[q * 8 + j], 1), :] = a_ref[j:j + 1, :]
    prob = prob_ref[...]
    a = a_v[...]
    hot = chosen_mask(idx_ref, n_exp, tok_count)
    pick = hot * prob
    pick_sum = jnp.sum(pick, axis=0, keepdims=True)
    gate = pick / pick_sum
    d_pick = (a - jnp.sum(a * gate, axis=0, keepdims=True)) / pick_sum
    d_prob = jnp.where(hot > 0.5, d_pick, 0.0) + aux_scale * frac_ref[...]
    dz = (prob * (d_prob - jnp.sum(prob * d_prob, axis=0, keepdims=True))).astype(BF16)
    dwr_ref[...] = dot_nn(dz, x_ref[...])
    dxr_ref[...] = lax.dot_general(dz, wr_ref[...], (((0,), (1,)), ((), ())), preferred_element_type=F32)


def cost(flops, nbytes):
    return pl.CostEstimate(flops=int(flops), bytes_accessed=int(nbytes), transcendentals=0)


def make_calls(capacity, tok_count, model_dim, ff_dim, n_exp):
    vmem = pl.BlockSpec(memory_space=pltpu.VMEM)
    smem = pl.BlockSpec(memory_space=pltpu.SMEM)
    hbm = pl.BlockSpec(memory_space=pl.ANY)
    shape = jax.ShapeDtypeStruct
    n_rows = 4 * capacity
    small = pl.BlockSpec((8, tok_count), lambda i: (0, 0))

    def gather(eid, x, dy, meta):
        rows = 2 * capacity
        full = pl.BlockSpec((tok_count, model_dim), lambda i: (0, 0))
        out = pl.BlockSpec((rows, model_dim), lambda i: (i, 0))
        slots = shape((8 * capacity, model_dim), BF16)
        vec = shape((8, tok_count), F32)
        return pl.pallas_call(
            functools.partial(gather_kernel, capacity), grid=(4,),
            out_shape=(slots, slots, shape((8 * capacity, 128), F32), vec, vec),
            in_specs=[smem, full, full, pl.BlockSpec((2 * n_exp, tok_count), lambda i: (0, 0))],
            out_specs=(out, out, pl.BlockSpec((rows, 128), lambda i: (i, 0)), small, small),
            compiler_params=params(dimension_semantics=("arbitrary",)),
            cost_estimate=cost(32 * capacity * tok_count * model_dim, 16e6), name="gather",
        )(eid, x, dy, meta)

    def experts(j, *args):
        slots = shape((4, capacity, model_dim), BF16)
        dw_in, dw_out = shape((model_dim, ff_dim), F32), shape((ff_dim, model_dim), F32)
        wide, narrow = pltpu.VMEM((n_rows, model_dim), BF16), pltpu.VMEM((n_rows, ff_dim), BF16)
        return pl.pallas_call(
            functools.partial(expert_kernel, j, capacity),
            out_shape=(slots, slots, shape((4, tok_count), F32), dw_in, dw_in, dw_out),
            in_specs=[hbm] * 12 + [vmem] * 4 + [hbm] * 3,
            out_specs=(hbm, hbm, vmem, hbm, hbm, hbm),
            scratch_shapes=[
                wide, wide, pltpu.VMEM((n_rows, 128), F32), pltpu.VMEM((4, tok_count), F32),
                pltpu.VMEM((model_dim, ff_dim), BF16), pltpu.VMEM((model_dim, ff_dim), BF16),
                pltpu.VMEM((ff_dim, model_dim), BF16), wide, wide, wide, narrow, narrow, narrow,
                pltpu.VMEM((model_dim, ff_dim), F32), pltpu.VMEM((model_dim, ff_dim), F32),
                pltpu.VMEM((ff_dim, model_dim), F32),
                pltpu.SemaphoreType.DMA((4, 3)), pltpu.SemaphoreType.DMA((3,)),
                pltpu.SemaphoreType.DMA((4, 2)), pltpu.SemaphoreType.DMA((3,)),
            ],
            compiler_params=params(56), cost_estimate=cost(18 * n_rows * model_dim * ff_dim, 20e6), name="experts",
        )(*args)

    def combine(t, *args):
        tile = 256
        pick = pl.BlockSpec((1, capacity, model_dim), lambda i: (t, 0, 0))
        out = pl.BlockSpec((tile, model_dim), lambda i: (i, 0))
        return pl.pallas_call(
            functools.partial(combine_kernel, capacity), grid=(tok_count // tile,),
            out_shape=(shape((tok_count, model_dim), F32),) * 2,
            in_specs=[pick] * 16 + [small] * 2, out_specs=(out, out),
            compiler_params=params(dimension_semantics=("arbitrary",)),
            cost_estimate=cost(32 * capacity * tok_count * model_dim, 20e6), name="combine",
        )(*args)

    return gather, experts, combine


def solution(mesh):
    n_dev = mesh.shape["ep"]

    def block_body(x_loc, w_router, wg_loc, wu_loc, wd_loc, idx_loc, dy_loc):
        tok_count, model_dim = x_loc.shape
        top_k = idx_loc.shape[1]
        n_exp = w_router.shape[1]
        ff_dim = wg_loc.shape[2]
        capacity = (5 * tok_count * top_k + 4 * n_exp - 1) // (4 * n_exp)
        n_total = tok_count * n_dev
        vmem = pl.BlockSpec(memory_space=pltpu.VMEM)
        smem = pl.BlockSpec(memory_space=pltpu.SMEM)
        shape = jax.ShapeDtypeStruct
        me = lax.axis_index("ep")
        core = me % 2
        column = (me // 2) % 4
        ring_pos = jnp.array([0, 1, 3, 2], jnp.int32)[me // 8]
        ring_arr = jnp.array(RING, jnp.int32)

        def expert_ids(col):
            dist = jnp.arange(4, dtype=jnp.int32)
            z_of = ring_arr[(ring_pos - dist + 4) % 4]
            base = z_of * 8 + col * 2
            return jnp.stack([base + core, base + 1 - core], axis=1).reshape(8)

        eid = expert_ids(column)
        eid_all = jnp.concatenate([eid, expert_ids(column ^ 1), expert_ids(column ^ 2), expert_ids(column ^ 3)])
        idx_t = idx_loc.T

        x_x, dy_x = send(x_loc, PERM_X), send(dy_loc, PERM_X)
        x_y, dy_y = send(x_loc, PERM_Y), send(dy_loc, PERM_Y)
        x_d, dy_d = send(x_x, PERM_Y), send(dy_y, PERM_X)
        xs_all = (x_loc, x_x, x_y, x_d)
        dys_all = (dy_loc, dy_x, dy_y, dy_d)

        mine = [(wg_loc[0], wu_loc[0], wd_loc[0])]
        for _ in range(3):
            mine.append(tuple(send(w, PERM_Z) for w in mine[-1]))
        other = [tuple(send(w, PERM_C) for w in ws) for ws in mine]

        prob, meta, stat = pl.pallas_call(
            functools.partial(route_kernel, capacity),
            out_shape=(shape((n_exp, tok_count), F32), shape((2 * n_exp, tok_count), F32), shape((n_exp, tok_count), F32)),
            in_specs=[vmem] * 3, out_specs=(vmem,) * 3, compiler_params=params(),
            cost_estimate=cost(4e9, 4e6), name="route",
        )(x_loc, w_router, idx_t)
        stat = lax.psum(stat, "ep")
        meta_x, meta_y = send(meta, PERM_X), send(meta, PERM_Y)
        meta_d = send(meta, PERM_D)
        load_frac = stat[:, 0:1] / (n_total * top_k)
        mean_prob = stat[:, tok_count - 1:] / n_total
        aux_loss = AUX_COEF * n_exp * jnp.sum(load_frac * mean_prob)

        gather, expert_call, combine_call = make_calls(capacity, tok_count, model_dim, ff_dim, n_exp)
        metas = (meta, meta_x, meta_y, meta_d)
        gathered = [gather(eid, x, dy, m) for x, dy, m in zip(xs_all, dys_all, metas)]
        xs, dr, ws, pos, gate = zip(*gathered)

        o_j, dx_j, a_j = [None] * 8, [None] * 8, [None] * 8
        travel = None
        for k in (1, 2, 3, 0):
            j = 2 * k + 1
            o_j[j], dx_j[j], a_j[j], *dw_other = expert_call(j, *xs, *dr, *ws, *pos, *other[k])
            dw_sib = [send(part, PERM_C) for part in dw_other]
            j = 2 * k
            o_j[j], dx_j[j], a_j[j], *dw_mine = expert_call(j, *xs, *dr, *ws, *pos, *mine[k])
            total = [own + sib for own, sib in zip(dw_mine, dw_sib)]
            if travel is not None:
                total = [part + came for part, came in zip(total, travel)]
            travel = [send(part, PERM_Z) for part in total] if k else total
        dw_gate, dw_up, dw_down = (part[None] for part in travel)

        def combine(t):
            return combine_call(t, *o_j, *dx_j, pos[t], gate[t])

        y_d, dx_d = combine(3)
        y_d_in, dx_d_in = send(y_d, PERM_X), send(dx_d, PERM_Y)
        y_x, dx_x = combine(1)
        y_x_in = send(y_x, PERM_X)
        y_y, dx_y = combine(2)
        dx_y_in = send(dx_y, PERM_Y)
        y_y_in = send(y_y + y_d_in, PERM_Y)
        dx_x_in = send(dx_x + dx_d_in, PERM_X)
        y_0, dx_0 = combine(0)

        def a_rows(t):
            return jnp.concatenate([a_j[j][t:t + 1] for j in range(8)], axis=0)

        a_in = [a_rows(0), send(a_rows(1), PERM_X), send(a_rows(2), PERM_Y), send(a_rows(3), PERM_D)]
        dwr_t, dx_r = pl.pallas_call(
            functools.partial(router_kernel, AUX_COEF * n_exp / n_total),
            out_shape=(shape((n_exp, model_dim), F32), shape((tok_count, model_dim), F32)),
            in_specs=[smem] + [vmem] * 9, out_specs=(vmem,) * 2,
            scratch_shapes=[pltpu.VMEM((n_exp, tok_count), F32)],
            compiler_params=params(), cost_estimate=cost(1e9, 8e6), name="router",
        )(eid_all, *a_in, prob, idx_t, load_frac, w_router, x_loc)
        dw_router = lax.psum(dwr_t, "ep").T
        y_loc = (y_0 + y_x_in + y_y_in).astype(BF16)
        dx_loc = (dx_0 + dx_y_in + dx_x_in + dx_r).astype(BF16)
        return y_loc, aux_loss, dx_loc, dw_router, dw_gate, dw_up, dw_down

    tok_spec = P("ep")
    return jax.shard_map(
        block_body,
        mesh=mesh,
        in_specs=(tok_spec, P(), tok_spec, tok_spec, tok_spec, tok_spec, tok_spec),
        out_specs=(tok_spec, P(), tok_spec, P(), tok_spec, tok_spec, tok_spec),
        check_vma=False,
    )
```

time: 2590 us -> 1140 us (0.44)
  blocking collectives: 945 us -> 0 us
  local copies, waits for them, and re-layouts: 431 us -> 13.8 us
  Pallas kernels: 0 us -> 331 us
  matrix products: 225 us -> 0 us
  waiting for transfers between devices: 847 us -> 640 us
    all_to_all x3 -> x0, waiting for transfers between devices: 799 us -> none  [the longest x1 412 us: local_block(): recv_x = lax.all_to_all(send_x, 'ep', 0, 1)]
    psum x1 -> x0, blocking collectives: 476 us -> none  [local_block(): load_stats = lax.psum(load_stats, 'ep')]
    all_to_all x1 -> x0, blocking collectives: 469 us -> none  [local_block(): recv_do = lax.all_to_all(send_do, 'ep', 0, 1)]
    gather x13 -> x1, local copies, waits for them, and re-layouts: 392 us -> 0.64 us  [expert_ids(): z_of = ring_arr[(ring_pos - dist + 4) % 4]]
    ppermute x0 -> x60, waiting for transfers between devices: none -> 364 us  [send(): return lax.ppermute(value, 'ep', perm)]
    pallas_call x0 -> x18, Pallas kernels: none -> 331 us  [the longest x8 179 us: experts(): pl.pallas_call(functools.partial(expert_kernel, j, capacity), out_shape=(...]
    psum x1 -> x2, waiting for transfers between devices: 48.5 us -> 276 us  [the longest x1 184 us: block_body(): stat = lax.psum(stat, 'ep')]
    dot_general x14 -> x0, matrix products: 225 us -> none  [the longest x1 34.7 us: local_block(): jnp.einsum('egcd,edf->egcf', recv_x, wu_loc, preferred_element_type=jnp.f...]
  transfers between devices with their start and end apart: 4 -> 62, of which waited for: 3 -> 23; matrix products, arithmetic and copies ran while one was open for 10% -> 8% of each run, Pallas kernels for 0% -> 29%
where the time goes in v1:
time: 1140 us; the launch traced here: 1130 us
  waiting for transfers between devices  640 us (56%)
  Pallas kernels  331 us (29%)
  other arithmetic  77.5 us (7%)
  starting transfers between devices  54.2 us (5%)
  between operations  16.6 us (1%)
  local copies, waits for them, and re-layouts  13.8 us (1%)
    ppermute x60, waiting for transfers between devices, send(): return lax.ppermute(value, 'ep', perm)  364 us
    psum x1, waiting for transfers between devices, block_body(): stat = lax.psum(stat, 'ep')  184 us
    pallas_call x8, Pallas kernels, experts(): pl.pallas_call(functools.partial(expert_kernel, j, capacity), out_shape=(...  179 us
    psum x1, waiting for transfers between devices, block_body(): dw_router = lax.psum(dwr_t, 'ep').T  92.4 us
    pallas_call x4, Pallas kernels, combine(): pl.pallas_call(functools.partial(combine_kernel, capacity), grid=(tok_cou...  80.8 us
    pallas_call x4, Pallas kernels, gather(): pl.pallas_call(functools.partial(gather_kernel, capacity), grid=(4,), out...  62.2 us
    ppermute x60, starting transfers between devices, send(): return lax.ppermute(value, 'ep', perm)  54.1 us
    add x6, other arithmetic, block_body(): total = [part + came for part, came in zip(total, travel)]  24.4 us
  transfers between devices with their start and end apart: 62, of which 23 were waited for; matrix products, arithmetic and copies ran while one was open for 8% of the time, Pallas kernels for 29%

profile of v1, /device:TPU:0, one launch (start us, length us, event | category | flops | bytes accessed | tf_op | source)
XLA Modules:
  0.0 1133.4 jit_solution(15994220459600248631)
XLA Ops:
  13.4 22.3 %collective-permute-done.12.refs_16_ = bf16[1024,512]{1,0:T(8,128)(2,1)} collective-permute-done((bf16[1024,512]{1,0:T(8,128)(2,1)}, bf16[1024,512]{1,0:T(8,128)(2,1)}, u32[]{:S(2)}, u32[]{:S(2)}) %collective-permute-start.12) | collective-permute-done | bytes 1048608 | tf_op jit(solution)/shard_map/ppermute | solution.py:34
  44.9 4.6 collective-permute-done.8.meta_ref
  51.0 7.0 collective-permute-done.13.refs_17_
  62.3 18.2 %collective-permute-done.14.refs_18_ = bf16[512,1024]{1,0:T(8,128)(2,1)S(1)} collective-permute-done((bf16[512,1024]{1,0:T(8,128)(2,1)}, bf16[512,1024]{1,0:T(8,128)(2,1)S(1)}, u32[]{:S(2)}, u32[]{:S(2)}) %collective-permute-start.14) | collective-permute-done | bytes 1048608 | tf_op jit(solution)/shard_map/ppermute | solution.py:34
  82.3 20.8 %collective-permute-done.18.refs_16_ = bf16[1024,512]{1,0:T(8,128)(2,1)} collective-permute-done((bf16[1024,512]{1,0:T(8,128)(2,1)}, bf16[1024,512]{1,0:T(8,128)(2,1)}, u32[]{:S(2)}, u32[]{:S(2)}) %collective-permute-start.18) | collective-permute-done | bytes 1048608 | tf_op jit(solution)/shard_map/ppermute | solution.py:34
  104.9 19.8 %collective-permute-done.19.refs_17_ = bf16[1024,512]{1,0:T(8,128)(2,1)} collective-permute-done((bf16[1024,512]{1,0:T(8,128)(2,1)S(1)}, bf16[1024,512]{1,0:T(8,128)(2,1)}, u32[]{:S(2)}, u32[]{:S(2)}) %collective-permute-start.19) | collective-permute-done | bytes 1048608 | tf_op jit(solution)/shard_map/ppermute | solution.py:34
  129.2 20.8 %collective-permute-done.20.refs_18_ = bf16[512,1024]{1,0:T(8,128)(2,1)} collective-permute-done((bf16[512,1024]{1,0:T(8,128)(2,1)S(1)}, bf16[512,1024]{1,0:T(8,128)(2,1)}, u32[]{:S(2)}, u32[]{:S(2)}) %collective-permute-start.20) | collective-permute-done | bytes 1048608 | tf_op jit(solution)/shard_map/ppermute | solution.py:34
  157.0 15.9 %gather.13 = (bf16[2560,1024]{1,0:T(8,128)(2,1)}, bf16[2560,1024]{1,0:T(8,128)(2,1)}, f32[2560,128]{1,0:T(8,128)}, f32[8,1024]{1,0:T(8,128)}, f32[8,1024]{1,0:T(8,128)}) custom-call(s32[8]{0:T(128)} %reshape.195.eid_ref, bf16[1024,1024]{1,0:T(8,128)(2,1)} %x_ref.5, bf16[1024,1024]{1,0:T(8,128)(2,1)} %dy_ref.1, f32[64,1024]{1,0:T(8,128)} %get-tuple-element.88.meta_ref), custom_call_target="tpu_custom_call" | custom-call | flops 10737418240 | bytes 16000000 | tf_op jit(solution)/shard_map/gather/pallas_call | solution.py:271
  173.0 15.5 %gather.15 = (bf16[2560,1024]{1,0:T(8,128)(2,1)}, bf16[2560,1024]{1,0:T(8,128)(2,1)}, f32[2560,128]{1,0:T(8,128)}, f32[8,1024]{1,0:T(8,128)}, f32[8,1024]{1,0:T(8,128)}) custom-call(s32[8]{0:T(128)} %reshape.195.eid_ref, bf16[1024,1024]{1,0:T(8,128)(2,1)} %collective-permute-done.3.x_ref, bf16[1024,1024]{1,0:T(8,128)(2,1)} %collective-permute-done.4.dy_ref, ...), custom_call_target="tpu_custom_call" | custom-call | flops 10737418240 | bytes 16000000 | tf_op jit(solution)/shard_map/gather/pallas_call | solution.py:271
  188.6 11.2 collective-permute-done.25.refs_17_
  199.7 19.9 %collective-permute-done.26.refs_18_ = bf16[512,1024]{1,0:T(8,128)(2,1)} collective-permute-done((bf16[512,1024]{1,0:T(8,128)(2,1)}, bf16[512,1024]{1,0:T(8,128)(2,1)}, u32[]{:S(2)}, u32[]{:S(2)}) %collective-permute-start.26) | collective-permute-done | bytes 1048608 | tf_op jit(solution)/shard_map/ppermute | solution.py:34
  219.6 15.4 %gather.14 = (bf16[2560,1024]{1,0:T(8,128)(2,1)}, bf16[2560,1024]{1,0:T(8,128)(2,1)}, f32[2560,128]{1,0:T(8,128)}, f32[8,1024]{1,0:T(8,128)}, f32[8,1024]{1,0:T(8,128)}) custom-call(s32[8]{0:T(128)} %reshape.195.eid_ref, bf16[1024,1024]{1,0:T(8,128)(2,1)} %collective-permute-done.x_ref, bf16[1024,1024]{1,0:T(8,128)(2,1)} %collective-permute-done.1.dy_ref, ...), custom_call_target="tpu_custom_call" | custom-call | flops 10737418240 | bytes 16000000 | tf_op jit(solution)/shard_map/gather/pallas_call | solution.py:271
  235.7 15.4 %gather.16 = (bf16[2560,1024]{1,0:T(8,128)(2,1)}, bf16[2560,1024]{1,0:T(8,128)(2,1)}, f32[2560,128]{1,0:T(8,128)}, f32[8,1024]{1,0:T(8,128)}, f32[8,1024]{1,0:T(8,128)}) custom-call(s32[8]{0:T(128)} %reshape.195.eid_ref, bf16[1024,1024]{1,0:T(8,128)(2,1)} %collective-permute-done.6.x_ref, bf16[1024,1024]{1,0:T(8,128)(2,1)} %collective-permute-done.7.dy_ref, ...), custom_call_target="tpu_custom_call" | custom-call | flops 10737418240 | bytes 16000000 | tf_op jit(solution)/shard_map/gather/pallas_call | solution.py:271
  252.1 22.5 %experts.15 = (bf16[4,320,1024]{2,1,0:T(8,128)(2,1)}, bf16[4,320,1024]{2,1,0:T(8,128)(2,1)}, f32[4,1024]{1,0:T(4,128)}, f32[1024,512]{1,0:T(8,128)}, f32[1024,512]{1,0:T(8,128)}, /*index=5*/f32[512,1024]{1,0:T(8,128)}) custom-call(bf16[2560,1024]{1,0:T(8,128)(2,1)} %get-tuple-element.89.refs_0_, bf16[2560,1024]{1,0:T(8,128)(2,1)} %get-tuple-element.90.refs_1_, ...), custom_call_target="tpu_custom_call" | custom-call | flops 12079595520 | bytes 20000000 | tf_op jit(solution)/shard_map/experts/pallas_call | solution.py:284
  276.0 22.3 %experts.14 = (bf16[4,320,1024]{2,1,0:T(8,128)(2,1)}, bf16[4,320,1024]{2,1,0:T(8,128)(2,1)}, f32[4,1024]{1,0:T(4,128)}, f32[1024,512]{1,0:T(8,128)}, f32[1024,512]{1,0:T(8,128)}, /*index=5*/f32[512,1024]{1,0:T(8,128)}) custom-call(bf16[2560,1024]{1,0:T(8,128)(2,1)} %get-tuple-element.89.refs_0_, bf16[2560,1024]{1,0:T(8,128)(2,1)} %get-tuple-element.90.refs_1_, ...), custom_call_target="tpu_custom_call" | custom-call | flops 12079595520 | bytes 20000000 | tf_op jit(solution)/shard_map/experts/pallas_call | solution.py:284
  299.3 22.2 %experts.8 = (bf16[4,320,1024]{2,1,0:T(8,128)(2,1)}, bf16[4,320,1024]{2,1,0:T(8,128)(2,1)}, f32[4,1024]{1,0:T(4,128)}, f32[1024,512]{1,0:T(8,128)}, f32[1024,512]{1,0:T(8,128)}, /*index=5*/f32[512,1024]{1,0:T(8,128)}) custom-call(bf16[2560,1024]{1,0:T(8,128)(2,1)} %get-tuple-element.89.refs_0_, bf16[2560,1024]{1,0:T(8,128)(2,1)} %get-tuple-element.90.refs_1_, ...), custom_call_target="tpu_custom_call" | custom-call | flops 12079595520 | bytes 20000000 | tf_op jit(solution)/shard_map/experts/pallas_call | solution.py:284
  322.8 22.2 %experts.13 = (bf16[4,320,1024]{2,1,0:T(8,128)(2,1)}, bf16[4,320,1024]{2,1,0:T(8,128)(2,1)}, f32[4,1024]{1,0:T(4,128)}, f32[1024,512]{1,0:T(8,128)}, f32[1024,512]{1,0:T(8,128)}, /*index=5*/f32[512,1024]{1,0:T(8,128)}) custom-call(bf16[2560,1024]{1,0:T(8,128)(2,1)} %get-tuple-element.89.refs_0_, bf16[2560,1024]{1,0:T(8,128)(2,1)} %get-tuple-element.90.refs_1_, ...), custom_call_target="tpu_custom_call" | custom-call | flops 12079595520 | bytes 20000000 | tf_op jit(solution)/shard_map/experts/pallas_call | solution.py:284
  346.0 22.5 %experts.12 = (bf16[4,320,1024]{2,1,0:T(8,128)(2,1)}, bf16[4,320,1024]{2,1,0:T(8,128)(2,1)}, f32[4,1024]{1,0:T(4,128)}, f32[1024,512]{1,0:T(8,128)}, f32[1024,512]{1,0:T(8,128)}, /*index=5*/f32[512,1024]{1,0:T(8,128)}) custom-call(bf16[2560,1024]{1,0:T(8,128)(2,1)} %get-tuple-element.89.refs_0_, bf16[2560,1024]{1,0:T(8,128)(2,1)} %get-tuple-element.90.refs_1_, ...), custom_call_target="tpu_custom_call" | custom-call | flops 12079595520 | bytes 20000000 | tf_op jit(solution)/shard_map/experts/pallas_call | solution.py:284
  368.5 22.3 %experts.10 = (bf16[4,320,1024]{2,1,0:T(8,128)(2,1)}, bf16[4,320,1024]{2,1,0:T(8,128)(2,1)}, f32[4,1024]{1,0:T(4,128)}, f32[1024,512]{1,0:T(8,128)}, f32[1024,512]{1,0:T(8,128)}, /*index=5*/f32[512,1024]{1,0:T(8,128)}) custom-call(bf16[2560,1024]{1,0:T(8,128)(2,1)} %get-tuple-element.89.refs_0_, bf16[2560,1024]{1,0:T(8,128)(2,1)} %get-tuple-element.90.refs_1_, ...), custom_call_target="tpu_custom_call" | custom-call | flops 12079595520 | bytes 20000000 | tf_op jit(solution)/shard_map/experts/pallas_call | solution.py:284
  391.9 22.3 %experts.11 = (bf16[4,320,1024]{2,1,0:T(8,128)(2,1)}, bf16[4,320,1024]{2,1,0:T(8,128)(2,1)}, f32[4,1024]{1,0:T(4,128)}, f32[1024,512]{1,0:T(8,128)}, f32[1024,512]{1,0:T(8,128)}, /*index=5*/f32[512,1024]{1,0:T(8,128)}) custom-call(bf16[2560,1024]{1,0:T(8,128)(2,1)} %get-tuple-element.89.refs_0_, bf16[2560,1024]{1,0:T(8,128)(2,1)} %get-tuple-element.90.refs_1_, ...), custom_call_target="tpu_custom_call" | custom-call | flops 12079595520 | bytes 20000000 | tf_op jit(solution)/shard_map/experts/pallas_call | solution.py:284
  415.8 22.7 %experts.9 = (bf16[4,320,1024]{2,1,0:T(8,128)(2,1)}, bf16[4,320,1024]{2,1,0:T(8,128)(2,1)}, f32[4,1024]{1,0:T(4,128)}, f32[1024,512]{1,0:T(8,128)}, f32[1024,512]{1,0:T(8,128)}, /*index=5*/f32[512,1024]{1,0:T(8,128)}) custom-call(bf16[2560,1024]{1,0:T(8,128)(2,1)} %get-tuple-element.89.refs_0_, bf16[2560,1024]{1,0:T(8,128)(2,1)} %get-tuple-element.90.refs_1_, ...), custom_call_target="tpu_custom_call" | custom-call | flops 12079595520 | bytes 20000000 | tf_op jit(solution)/shard_map/experts/pallas_call | solution.py:284
  458.0 20.2 %combine.7 = (f32[1024,1024]{1,0:T(8,128)}, f32[1024,1024]{1,0:T(8,128)}) custom-call(bf16[4,320,1024]{2,1,0:T(8,128)(2,1)} %get-tuple-element.105.refs_0_, bf16[4,320,1024]{2,1,0:T(8,128)(2,1)} %get-tuple-element.106.refs_1_, bf16[4,320,1024]{2,1,0:T(8,128)(2,1)} %get-tuple-element.107.refs_2_, bf16[4,320,1024]{2,1,0:T(8,128)(2,1)} %get-tuple-element.108.refs_3_, ...), custom_call_target="tpu_custom_call" | custom-call | flops 10737418240 | bytes 20000000 | tf_op jit(solution)/shard_map/combine/pallas_call | solution.py:305
  492.0 20.4 %combine.6 = (f32[1024,1024]{1,0:T(8,128)}, f32[1024,1024]{1,0:T(8,128)}) custom-call(bf16[4,320,1024]{2,1,0:T(8,128)(2,1)} %get-tuple-element.105.refs_0_, bf16[4,320,1024]{2,1,0:T(8,128)(2,1)} %get-tuple-element.106.refs_1_, bf16[4,320,1024]{2,1,0:T(8,128)(2,1)} %get-tuple-element.107.refs_2_, bf16[4,320,1024]{2,1,0:T(8,128)(2,1)} %get-tuple-element.108.refs_3_, ...), custom_call_target="tpu_custom_call" | custom-call | flops 10737418240 | bytes 20000000 | tf_op jit(solution)/shard_map/combine/pallas_call | solution.py:305
  513.0 3.6 add.370
  516.6 17.5 %collective-permute-done.43 = f32[1024,512]{1,0:T(8,128)} collective-permute-done((f32[1024,512]{1,0:T(8,128)}, f32[1024,512]{1,0:T(8,128)}, u32[]{:S(2)}, u32[]{:S(2)}) %collective-permute-start.43) | collective-permute-done | bytes 2097184 | tf_op jit(solution)/shard_map/ppermute | solution.py:34
  534.9 4.3 add_add_fusion.4
  539.2 39.8 %collective-permute-done.50 = f32[1024,512]{1,0:T(8,128)} collective-permute-done((f32[1024,512]{1,0:T(8,128)}, f32[1024,512]{1,0:T(8,128)}, u32[]{:S(2)}, u32[]{:S(2)}) %collective-permute-start.50) | collective-permute-done | bytes 2097184 | tf_op jit(solution)/shard_map/ppermute | solution.py:34
  579.9 20.1 %combine.5 = (f32[1024,1024]{1,0:T(8,128)}, f32[1024,1024]{1,0:T(8,128)}) custom-call(bf16[4,320,1024]{2,1,0:T(8,128)(2,1)} %get-tuple-element.105.refs_0_, bf16[4,320,1024]{2,1,0:T(8,128)(2,1)} %get-tuple-element.106.refs_1_, bf16[4,320,1024]{2,1,0:T(8,128)(2,1)} %get-tuple-element.107.refs_2_, bf16[4,320,1024]{2,1,0:T(8,128)(2,1)} %get-tuple-element.108.refs_3_, ...), custom_call_target="tpu_custom_call" | custom-call | flops 10737418240 | bytes 20000000 | tf_op jit(solution)/shard_map/combine/pallas_call | solution.py:305
  600.5 7.0 add.332
  608.1 5.3 add.335
  613.4 10.6 collective-permute-done.57
  625.8 4.4 add_add_fusion.2
  630.3 33.0 %collective-permute-done.33 = f32[1024,1024]{1,0:T(8,128)} collective-permute-done((f32[1024,1024]{1,0:T(8,128)}, f32[1024,1024]{1,0:T(8,128)}, u32[]{:S(2)}, u32[]{:S(2)}) %collective-permute-start.33) | collective-permute-done | bytes 4194336 | tf_op jit(solution)/shard_map/ppermute | solution.py:34
  664.0 4.2 add_add_fusion
  671.8 183.8 %all-reduce.3.cloned.1.call-done = f32[32,1024]{1,0:T(8,128)} async-done(((f32[32,1024]{1,0:T(8,128)}), f32[32,1024]{1,0:T(8,128)}) %all-reduce.3.cloned.1.call-update) | async-done | bytes 131088 | tf_op jit(solution)/shard_map/psum | solution.py:362
  858.8 20.1 %combine.4 = (f32[1024,1024]{1,0:T(8,128)}, f32[1024,1024]{1,0:T(8,128)}) custom-call(bf16[4,320,1024]{2,1,0:T(8,128)(2,1)} %get-tuple-element.105.refs_0_, bf16[4,320,1024]{2,1,0:T(8,128)(2,1)} %get-tuple-element.106.refs_1_, bf16[4,320,1024]{2,1,0:T(8,128)(2,1)} %get-tuple-element.107.refs_2_, bf16[4,320,1024]{2,1,0:T(8,128)(2,1)} %get-tuple-element.108.refs_3_, ...), custom_call_target="tpu_custom_call" | custom-call | flops 10737418240 | bytes 20000000 | tf_op jit(solution)/shard_map/combine/pallas_call | solution.py:305
  879.0 5.2 router.1
  884.2 4.4 add_add_fusion.5
  894.9 3.8 add_add_fusion.1
  899.7 6.2 add_convert_fusion.1
  906.0 6.6 add_convert_fusion
  912.6 26.3 %collective-permute-done.45 = f32[1024,512]{1,0:T(8,128)} collective-permute-done((f32[1024,512]{1,0:T(8,128)}, f32[1024,512]{1,0:T(8,128)}, u32[]{:S(2)}, u32[]{:S(2)}) %collective-permute-start.45) | collective-permute-done | bytes 2097184 | tf_op jit(solution)/shard_map/ppermute | solution.py:34
  938.9 4.4 add_bitcast_fusion.2
  943.4 40.5 %collective-permute-done.52 = f32[1024,512]{1,0:T(8,128)} collective-permute-done((f32[1024,512]{1,0:T(8,128)S(1)}, f32[1024,512]{1,0:T(8,128)}, u32[]{:S(2)}, u32[]{:S(2)}) %collective-permute-start.52) | collective-permute-done | bytes 2097184 | tf_op jit(solution)/shard_map/ppermute | solution.py:34
  983.9 4.4 add_bitcast_fusion.1
  988.3 38.7 %collective-permute-done.59 = f32[512,1024]{1,0:T(8,128)} collective-permute-done((f32[512,1024]{1,0:T(8,128)}, f32[512,1024]{1,0:T(8,128)}, u32[]{:S(2)}, u32[]{:S(2)}) %collective-permute-start.59) | collective-permute-done | bytes 2097184 | tf_op jit(solution)/shard_map/ppermute | solution.py:34
  1027.0 4.2 add_bitcast_fusion
  1031.2 92.4 %all-reduce.5.cloned.1.call-done = f32[1024,32]{0,1:T(8,128)} async-done(((f32[1024,32]{0,1:T(8,128)}), f32[1024,32]{0,1:T(8,128)}) %all-reduce.5.cloned.1.call-update) | async-done | bytes 131088 | tf_op jit(solution)/shard_map/psum | solution.py:412
  (237 shorter events, 99.2 us)
Async XLA Ops:
  7.2 848.4 %all-reduce.3.cloned.1.call-start = ((), (), s32[]{:S(2)}) async-start(), calls=%async_computation | async-start | bytes 262144 | tf_op jit(solution)/shard_map/psum | solution.py:362
  10.3 47.7 %collective-permute-start.13 = (bf16[1024,512]{1,0:T(8,128)(2,1)}, bf16[1024,512]{1,0:T(8,128)(2,1)S(1)}, u32[]{:S(2)}, u32[]{:S(2)}) collective-permute-start(bf16[1024,512]{1,0:T(8,128)(2,1)} %bitcast.33), channel_id=1, source_target_pairs={{0,8},{1,9},{2,10},{3,11},{4,12},{5,13},{6,14},{7,15},{8,24},{9,25... | collective-permute-start | bytes 3145736 | tf_op jit(solution)/shard_map/ppermute | solution.py:34
  12.9 67.6 %collective-permute-start.14 = (bf16[512,1024]{1,0:T(8,128)(2,1)}, bf16[512,1024]{1,0:T(8,128)(2,1)S(1)}, u32[]{:S(2)}, u32[]{:S(2)}) collective-permute-start(bf16[512,1024]{1,0:T(8,128)(2,1)} %bitcast.36), channel_id=1, source_target_pairs={{0,8},{1,9},{2,10},{3,11},{4,12},{5,13},{6,14},{7,15},{8,24},{9,25... | collective-permute-start | bytes 3145736 | tf_op jit(solution)/shard_map/ppermute | solution.py:34
  35.7 67.4 %collective-permute-start.18 = (bf16[1024,512]{1,0:T(8,128)(2,1)}, bf16[1024,512]{1,0:T(8,128)(2,1)}, u32[]{:S(2)}, u32[]{:S(2)}) collective-permute-start(bf16[1024,512]{1,0:T(8,128)(2,1)} %collective-permute-done.12.refs_16_), channel_id=1, source_target_pairs={{0,8},{1,9},{2,10},{3,11},{4,12},{5,13},{6,14},{7,15},{8,24},{9,25... | collective-permute-start | bytes 3145736 | tf_op jit(solution)/shard_map/ppermute | solution.py:34
  58.0 66.7 %collective-permute-start.19 = (bf16[1024,512]{1,0:T(8,128)(2,1)S(1)}, bf16[1024,512]{1,0:T(8,128)(2,1)}, u32[]{:S(2)}, u32[]{:S(2)}) collective-permute-start(bf16[1024,512]{1,0:T(8,128)(2,1)S(1)} %collective-permute-done.13.refs_17_), channel_id=1, source_target_pairs={{0,8},{1,9},{2,10},{3,11},{4,12},{5,13},{6,14},{7,15},{8,24},{9,25... | collective-permute-start | bytes 3145736 | tf_op jit(solution)/shard_map/ppermute | solution.py:34
  59.2 91.2 %collective-permute-start.4 = (bf16[1024,1024]{1,0:T(8,128)(2,1)}, bf16[1024,1024]{1,0:T(8,128)(2,1)}, u32[]{:S(2)}, u32[]{:S(2)}) collective-permute-start(bf16[1024,1024]{1,0:T(8,128)(2,1)} %dy_ref.1), channel_id=1, source_target_pairs={{0,4},{1,5},{2,6},{3,7},{4,0},{5,1},{6,2},{7,3},{8,12},{9,13},{10,... | collective-permute-start | bytes 6291464 | tf_op jit(solution)/shard_map/ppermute | solution.py:34
  60.8 93.2 %collective-permute-start.1 = (bf16[1024,1024]{1,0:T(8,128)(2,1)}, bf16[1024,1024]{1,0:T(8,128)(2,1)}, u32[]{:S(2)}, u32[]{:S(2)}) collective-permute-start(bf16[1024,1024]{1,0:T(8,128)(2,1)} %dy_ref.1), channel_id=1, source_target_pairs={{0,2},{1,3},{2,0},{3,1},{4,6},{5,7},{6,4},{7,5},{8,10},{9,11},{10,... | collective-permute-start | bytes 6291464 | tf_op jit(solution)/shard_map/ppermute | solution.py:34
  80.5 73.5 %collective-permute-start = (bf16[1024,1024]{1,0:T(8,128)(2,1)}, bf16[1024,1024]{1,0:T(8,128)(2,1)}, u32[]{:S(2)}, u32[]{:S(2)}) collective-permute-start(bf16[1024,1024]{1,0:T(8,128)(2,1)} %x_ref.5), channel_id=1, source_target_pairs={{0,2},{1,3},{2,0},{3,1},{4,6},{5,7},{6,4},{7,5},{8,10},{9,11},{10,... | collective-permute-start | bytes 6291464 | tf_op jit(solution)/shard_map/ppermute | solution.py:34
  103.1 52.5 %collective-permute-start.3 = (bf16[1024,1024]{1,0:T(8,128)(2,1)}, bf16[1024,1024]{1,0:T(8,128)(2,1)}, u32[]{:S(2)}, u32[]{:S(2)}) collective-permute-start(bf16[1024,1024]{1,0:T(8,128)(2,1)} %x_ref.5), channel_id=1, source_target_pairs={{0,4},{1,5},{2,6},{3,7},{4,0},{5,1},{6,2},{7,3},{8,12},{9,13},{10,... | collective-permute-start | bytes 6291464 | tf_op jit(solution)/shard_map/ppermute | solution.py:34
  150.0 38.4 %collective-permute-start.24 = (bf16[1024,512]{1,0:T(8,128)(2,1)}, bf16[1024,512]{1,0:T(8,128)(2,1)}, u32[]{:S(2)}, u32[]{:S(2)}) collective-permute-start(bf16[1024,512]{1,0:T(8,128)(2,1)} %collective-permute-done.18.refs_16_), channel_id=1, source_target_pairs={{0,8},{1,9},{2,10},{3,11},{4,12},{5,13},{6,14},{7,15},{8,24},{9,25... | collective-permute-start | bytes 3145736 | tf_op jit(solution)/shard_map/ppermute | solution.py:34
  150.5 49.3 %collective-permute-start.25 = (bf16[1024,512]{1,0:T(8,128)(2,1)}, bf16[1024,512]{1,0:T(8,128)(2,1)}, u32[]{:S(2)}, u32[]{:S(2)}) collective-permute-start(bf16[1024,512]{1,0:T(8,128)(2,1)} %collective-permute-done.19.refs_17_), channel_id=1, source_target_pairs={{0,8},{1,9},{2,10},{3,11},{4,12},{5,13},{6,14},{7,15},{8,24},{9,25... | collective-permute-start | bytes 3145736 | tf_op jit(solution)/shard_map/ppermute | solution.py:34
  154.0 65.7 %collective-permute-start.26 = (bf16[512,1024]{1,0:T(8,128)(2,1)}, bf16[512,1024]{1,0:T(8,128)(2,1)}, u32[]{:S(2)}, u32[]{:S(2)}) collective-permute-start(bf16[512,1024]{1,0:T(8,128)(2,1)} %collective-permute-done.20.refs_18_), channel_id=1, source_target_pairs={{0,8},{1,9},{2,10},{3,11},{4,12},{5,13},{6,14},{7,15},{8,24},{9,25... | collective-permute-start | bytes 3145736 | tf_op jit(solution)/shard_map/ppermute | solution.py:34
  154.0 81.1 %collective-permute-start.7 = (bf16[1024,1024]{1,0:T(8,128)(2,1)}, bf16[1024,1024]{1,0:T(8,128)(2,1)}, u32[]{:S(2)}, u32[]{:S(2)}) collective-permute-start(bf16[1024,1024]{1,0:T(8,128)(2,1)} %collective-permute-done.4.dy_ref), channel_id=1, source_target_pairs={{0,2},{1,3},{2,0},{3,1},{4,6},{5,7},{6,4},{7,5},{8,10},{9,11},{10,... | collective-permute-start | bytes 6291464 | tf_op jit(solution)/shard_map/ppermute | solution.py:34
  155.5 80.1 %collective-permute-start.6 = (bf16[1024,1024]{1,0:T(8,128)(2,1)}, bf16[1024,1024]{1,0:T(8,128)(2,1)}, u32[]{:S(2)}, u32[]{:S(2)}) collective-permute-start(bf16[1024,1024]{1,0:T(8,128)(2,1)} %collective-permute-done.x_ref), channel_id=1, source_target_pairs={{0,4},{1,5},{2,6},{3,7},{4,0},{5,1},{6,2},{7,3},{8,12},{9,13},{10,... | collective-permute-start | bytes 6291464 | tf_op jit(solution)/shard_map/ppermute | solution.py:34
  188.5 62.7 %collective-permute-start.27 = (bf16[1024,512]{1,0:T(8,128)(2,1)}, bf16[1024,512]{1,0:T(8,128)(2,1)}, u32[]{:S(2)}, u32[]{:S(2)}) collective-permute-start(bf16[1024,512]{1,0:T(8,128)(2,1)} %collective-permute-done.24.refs_16_), channel_id=1, source_target_pairs={{0,1},{1,0},{2,3},{3,2},{4,5},{5,4},{6,7},{7,6},{8,9},{9,8},{10,11... | collective-permute-start | bytes 3145736 | tf_op jit(solution)/shard_map/ppermute | solution.py:34
  199.7 51.8 %collective-permute-start.28 = (bf16[1024,512]{1,0:T(8,128)(2,1)}, bf16[1024,512]{1,0:T(8,128)(2,1)}, u32[]{:S(2)}, u32[]{:S(2)}) collective-permute-start(bf16[1024,512]{1,0:T(8,128)(2,1)} %collective-permute-done.25.refs_17_), channel_id=1, source_target_pairs={{0,1},{1,0},{2,3},{3,2},{4,5},{5,4},{6,7},{7,6},{8,9},{9,8},{10,11... | collective-permute-start | bytes 3145736 | tf_op jit(solution)/shard_map/ppermute | solution.py:34
  235.1 179.1 %collective-permute-start.9 = (bf16[1024,512]{1,0:T(8,128)(2,1)S(1)}, bf16[1024,512]{1,0:T(8,128)(2,1)}, u32[]{:S(2)}, u32[]{:S(2)}) collective-permute-start(bf16[1024,512]{1,0:T(8,128)(2,1)S(1)} %bitcast.32), channel_id=1, source_target_pairs={{0,1},{1,0},{2,3},{3,2},{4,5},{5,4},{6,7},{7,6},{8,9},{9,8},{10,11... | collective-permute-start | bytes 3145736 | tf_op jit(solution)/shard_map/ppermute | solution.py:34
  235.6 178.8 %collective-permute-start.10 = (bf16[1024,512]{1,0:T(8,128)(2,1)S(1)}, bf16[1024,512]{1,0:T(8,128)(2,1)}, u32[]{:S(2)}, u32[]{:S(2)}) collective-permute-start(bf16[1024,512]{1,0:T(8,128)(2,1)S(1)} %bitcast.35), channel_id=1, source_target_pairs={{0,1},{1,0},{2,3},{3,2},{4,5},{5,4},{6,7},{7,6},{8,9},{9,8},{10,11... | collective-permute-start | bytes 3145736 | tf_op jit(solution)/shard_map/ppermute | solution.py:34
  251.1 70.4 %collective-permute-start.21 = (bf16[1024,512]{1,0:T(8,128)(2,1)}, bf16[1024,512]{1,0:T(8,128)(2,1)S(1)}, u32[]{:S(2)}, u32[]{:S(2)}) collective-permute-start(bf16[1024,512]{1,0:T(8,128)(2,1)} %collective-permute-done.18.refs_16_), channel_id=1, source_target_pairs={{0,1},{1,0},{2,3},{3,2},{4,5},{5,4},{6,7},{7,6},{8,9},{9,8},{10,11... | collective-permute-start | bytes 3145736 | tf_op jit(solution)/shard_map/ppermute | solution.py:34
  251.6 70.1 %collective-permute-start.22 = (bf16[1024,512]{1,0:T(8,128)(2,1)}, bf16[1024,512]{1,0:T(8,128)(2,1)S(1)}, u32[]{:S(2)}, u32[]{:S(2)}) collective-permute-start(bf16[1024,512]{1,0:T(8,128)(2,1)} %collective-permute-done.19.refs_17_), channel_id=1, source_target_pairs={{0,1},{1,0},{2,3},{3,2},{4,5},{5,4},{6,7},{7,6},{8,9},{9,8},{10,11... | collective-permute-start | bytes 3145736 | tf_op jit(solution)/shard_map/ppermute | solution.py:34
  251.7 70.5 %collective-permute-start.23 = (bf16[512,1024]{1,0:T(8,128)(2,1)}, bf16[512,1024]{1,0:T(8,128)(2,1)}, u32[]{:S(2)}, u32[]{:S(2)}) collective-permute-start(bf16[512,1024]{1,0:T(8,128)(2,1)} %collective-permute-done.20.refs_18_), channel_id=1, source_target_pairs={{0,1},{1,0},{2,3},{3,2},{4,5},{5,4},{6,7},{7,6},{8,9},{9,8},{10,11... | collective-permute-start | bytes 3145736 | tf_op jit(solution)/shard_map/ppermute | solution.py:34
  321.5 69.3 %collective-permute-start.15 = (bf16[1024,512]{1,0:T(8,128)(2,1)}, bf16[1024,512]{1,0:T(8,128)(2,1)S(1)}, u32[]{:S(2)}, u32[]{:S(2)}) collective-permute-start(bf16[1024,512]{1,0:T(8,128)(2,1)} %collective-permute-done.12.refs_16_), channel_id=1, source_target_pairs={{0,1},{1,0},{2,3},{3,2},{4,5},{5,4},{6,7},{7,6},{8,9},{9,8},{10,11... | collective-permute-start | bytes 3145736 | tf_op jit(solution)/shard_map/ppermute | solution.py:34
  321.7 69.5 %collective-permute-start.16 = (bf16[1024,512]{1,0:T(8,128)(2,1)S(1)}, bf16[1024,512]{1,0:T(8,128)(2,1)}, u32[]{:S(2)}, u32[]{:S(2)}) collective-permute-start(bf16[1024,512]{1,0:T(8,128)(2,1)S(1)} %copy-done.25), channel_id=1, source_target_pairs={{0,1},{1,0},{2,3},{3,2},{4,5},{5,4},{6,7},{7,6},{8,9},{9,8},{10,11... | collective-permute-start | bytes 3145736 | tf_op jit(solution)/shard_map/ppermute | solution.py:34
  322.2 69.3 %collective-permute-start.17 = (bf16[512,1024]{1,0:T(8,128)(2,1)S(1)}, bf16[512,1024]{1,0:T(8,128)(2,1)}, u32[]{:S(2)}, u32[]{:S(2)}) collective-permute-start(bf16[512,1024]{1,0:T(8,128)(2,1)S(1)} %collective-permute-done.14.refs_18_), channel_id=1, source_target_pairs={{0,1},{1,0},{2,3},{3,2},{4,5},{5,4},{6,7},{7,6},{8,9},{9,8},{10,11... | collective-permute-start | bytes 3145736 | tf_op jit(solution)/shard_map/ppermute | solution.py:34
  391.2 61.1 %collective-permute-start.40 = (f32[1024,512]{1,0:T(8,128)}, f32[1024,512]{1,0:T(8,128)}, u32[]{:S(2)}, u32[]{:S(2)}) collective-permute-start(f32[1024,512]{1,0:T(8,128)} %get-tuple-element.148), channel_id=1, source_target_pairs={{0,1},{1,0},{2,3},{3,2},{4,5},{5,4},{6,7},{7,6},{8,9},{9,8},{10,11... | collective-permute-start | bytes 6291464 | tf_op jit(solution)/shard_map/ppermute | solution.py:34
  391.5 61.4 %collective-permute-start.47 = (f32[1024,512]{1,0:T(8,128)}, f32[1024,512]{1,0:T(8,128)}, u32[]{:S(2)}, u32[]{:S(2)}) collective-permute-start(f32[1024,512]{1,0:T(8,128)} %get-tuple-element.156), channel_id=1, source_target_pairs={{0,1},{1,0},{2,3},{3,2},{4,5},{5,4},{6,7},{7,6},{8,9},{9,8},{10,11... | collective-permute-start | bytes 6291464 | tf_op jit(solution)/shard_map/ppermute | solution.py:34
  414.2 38.8 %collective-permute-start.54 = (f32[512,1024]{1,0:T(8,128)}, f32[512,1024]{1,0:T(8,128)S(1)}, u32[]{:S(2)}, u32[]{:S(2)}) collective-permute-start(f32[512,1024]{1,0:T(8,128)} %get-tuple-element.164), channel_id=1, source_target_pairs={{0,1},{1,0},{2,3},{3,2},{4,5},{5,4},{6,7},{7,6},{8,9},{9,8},{10,11... | collective-permute-start | bytes 6291464 | tf_op jit(solution)/shard_map/ppermute | solution.py:34
  414.5 38.9 %collective-permute-start.41 = (f32[1024,512]{1,0:T(8,128)}, f32[1024,512]{1,0:T(8,128)}, u32[]{:S(2)}, u32[]{:S(2)}) collective-permute-start(f32[1024,512]{1,0:T(8,128)} %get-tuple-element.150), channel_id=1, source_target_pairs={{0,1},{1,0},{2,3},{3,2},{4,5},{5,4},{6,7},{7,6},{8,9},{9,8},{10,11... | collective-permute-start | bytes 6291464 | tf_op jit(solution)/shard_map/ppermute | solution.py:34
  453.4 35.2 %collective-permute-start.56 = (f32[512,1024]{1,0:T(8,128)}, f32[512,1024]{1,0:T(8,128)}, u32[]{:S(2)}, u32[]{:S(2)}) collective-permute-start(f32[512,1024]{1,0:T(8,128)} %get-tuple-element.168), channel_id=1, source_target_pairs={{0,1},{1,0},{2,3},{3,2},{4,5},{5,4},{6,7},{7,6},{8,9},{9,8},{10,11... | collective-permute-start | bytes 6291464 | tf_op jit(solution)/shard_map/ppermute | solution.py:34
  456.7 55.7 %collective-permute-start.39 = (f32[1024,512]{1,0:T(8,128)}, f32[1024,512]{1,0:T(8,128)}, u32[]{:S(2)}, u32[]{:S(2)}) collective-permute-start(f32[1024,512]{1,0:T(8,128)} %get-tuple-element.146), channel_id=1, source_target_pairs={{0,1},{1,0},{2,3},{3,2},{4,5},{5,4},{6,7},{7,6},{8,9},{9,8},{10,11... | collective-permute-start | bytes 6291464 | tf_op jit(solution)/shard_map/ppermute | solution.py:34
  478.3 121.7 %collective-permute-start.31 = (f32[1024,1024]{1,0:T(8,128)}, f32[1024,1024]{1,0:T(8,128)}, u32[]{:S(2)}, u32[]{:S(2)}) collective-permute-start(f32[1024,1024]{1,0:T(8,128)} %get-tuple-element.128), channel_id=1, source_target_pairs={{0,2},{1,3},{2,0},{3,1},{4,6},{5,7},{6,4},{7,5},{8,10},{9,11},{10,... | collective-permute-start | bytes 12582920 | tf_op jit(solution)/shard_map/ppermute | solution.py:34
  479.3 128.2 %collective-permute-start.34 = (f32[1024,1024]{1,0:T(8,128)}, f32[1024,1024]{1,0:T(8,128)}, u32[]{:S(2)}, u32[]{:S(2)}) collective-permute-start(f32[1024,1024]{1,0:T(8,128)} %get-tuple-element.133), channel_id=1, source_target_pairs={{0,4},{1,5},{2,6},{3,7},{4,0},{5,1},{6,2},{7,3},{8,12},{9,13},{10,... | collective-permute-start | bytes 12582920 | tf_op jit(solution)/shard_map/ppermute | solution.py:34
  484.4 49.7 %collective-permute-start.43 = (f32[1024,512]{1,0:T(8,128)}, f32[1024,512]{1,0:T(8,128)}, u32[]{:S(2)}, u32[]{:S(2)}) collective-permute-start(f32[1024,512]{1,0:T(8,128)} %add.356), channel_id=1, source_target_pairs={{0,8},{1,9},{2,10},{3,11},{4,12},{5,13},{6,14},{7,15},{8,24},{9,25... | collective-permute-start | bytes 6291464 | tf_op jit(solution)/shard_map/ppermute | solution.py:34
  488.6 90.5 %collective-permute-start.50 = (f32[1024,512]{1,0:T(8,128)}, f32[1024,512]{1,0:T(8,128)}, u32[]{:S(2)}, u32[]{:S(2)}) collective-permute-start(f32[1024,512]{1,0:T(8,128)} %add.363), channel_id=1, source_target_pairs={{0,8},{1,9},{2,10},{3,11},{4,12},{5,13},{6,14},{7,15},{8,24},{9,25... | collective-permute-start | bytes 6291464 | tf_op jit(solution)/shard_map/ppermute | solution.py:34
  512.4 150.8 %collective-permute-start.33 = (f32[1024,1024]{1,0:T(8,128)}, f32[1024,1024]{1,0:T(8,128)}, u32[]{:S(2)}, u32[]{:S(2)}) collective-permute-start(f32[1024,1024]{1,0:T(8,128)} %get-tuple-element.131), channel_id=1, source_target_pairs={{0,4},{1,5},{2,6},{3,7},{4,0},{5,1},{6,2},{7,3},{8,12},{9,13},{10,... | collective-permute-start | bytes 12582920 | tf_op jit(solution)/shard_map/ppermute | solution.py:34
  534.1 89.9 %collective-permute-start.57 = (f32[512,1024]{1,0:T(8,128)}, f32[512,1024]{1,0:T(8,128)}, u32[]{:S(2)}, u32[]{:S(2)}) collective-permute-start(f32[512,1024]{1,0:T(8,128)} %add.370), channel_id=1, source_target_pairs={{0,8},{1,9},{2,10},{3,11},{4,12},{5,13},{6,14},{7,15},{8,24},{9,25... | collective-permute-start | bytes 6291464 | tf_op jit(solution)/shard_map/ppermute | solution.py:34
  579.1 90.5 %collective-permute-start.44 = (f32[1024,512]{1,0:T(8,128)}, f32[1024,512]{1,0:T(8,128)}, u32[]{:S(2)}, u32[]{:S(2)}) collective-permute-start(f32[1024,512]{1,0:T(8,128)} %add_add_fusion.4), channel_id=1, source_target_pairs={{0,8},{1,9},{2,10},{3,11},{4,12},{5,13},{6,14},{7,15},{8,24},{9,25... | collective-permute-start | bytes 6291464 | tf_op jit(solution)/shard_map/ppermute | solution.py:34
  600.0 293.4 %collective-permute-start.30 = (f32[1024,1024]{1,0:T(8,128)}, f32[1024,1024]{1,0:T(8,128)}, u32[]{:S(2)}, u32[]{:S(2)}) collective-permute-start(f32[1024,1024]{1,0:T(8,128)} %get-tuple-element.124), channel_id=1, source_target_pairs={{0,2},{1,3},{2,0},{3,1},{4,6},{5,7},{6,4},{7,5},{8,10},{9,11},{10,... | collective-permute-start | bytes 12582920 | tf_op jit(solution)/shard_map/ppermute | solution.py:34
  607.5 291.2 %collective-permute-start.32 = (f32[1024,1024]{1,0:T(8,128)}, f32[1024,1024]{1,0:T(8,128)}, u32[]{:S(2)}, u32[]{:S(2)}) collective-permute-start(f32[1024,1024]{1,0:T(8,128)} %add.332), channel_id=1, source_target_pairs={{0,4},{1,5},{2,6},{3,7},{4,0},{5,1},{6,2},{7,3},{8,12},{9,13},{10,... | collective-permute-start | bytes 12582920 | tf_op jit(solution)/shard_map/ppermute | solution.py:34
  624.0 274.9 %collective-permute-start.35 = (f32[1024,1024]{1,0:T(8,128)}, f32[1024,1024]{1,0:T(8,128)}, u32[]{:S(2)}, u32[]{:S(2)}) collective-permute-start(f32[1024,1024]{1,0:T(8,128)} %add.335), channel_id=1, source_target_pairs={{0,2},{1,3},{2,0},{3,1},{4,6},{5,7},{6,4},{7,5},{8,10},{9,11},{10,... | collective-permute-start | bytes 12582920 | tf_op jit(solution)/shard_map/ppermute | solution.py:34
  624.6 499.0 %all-reduce.5.cloned.1.call-start = ((), (), s32[]{:S(2)}) async-start(), calls=%async_computation.1 | async-start | bytes 262144 | tf_op jit(solution)/shard_map/psum | solution.py:412
  663.2 225.4 %collective-permute-start.51 = (f32[1024,512]{1,0:T(8,128)}, f32[1024,512]{1,0:T(8,128)}, u32[]{:S(2)}, u32[]{:S(2)}) collective-permute-start(f32[1024,512]{1,0:T(8,128)} %add_add_fusion.2), channel_id=1, source_target_pairs={{0,8},{1,9},{2,10},{3,11},{4,12},{5,13},{6,14},{7,15},{8,24},{9,25... | collective-permute-start | bytes 6291464 | tf_op jit(solution)/shard_map/ppermute | solution.py:34
  669.5 223.9 %collective-permute-start.58 = (f32[512,1024]{1,0:T(8,128)}, f32[512,1024]{1,0:T(8,128)}, u32[]{:S(2)}, u32[]{:S(2)}) collective-permute-start(f32[512,1024]{1,0:T(8,128)} %add_add_fusion), channel_id=1, source_target_pairs={{0,8},{1,9},{2,10},{3,11},{4,12},{5,13},{6,14},{7,15},{8,24},{9,25... | collective-permute-start | bytes 6291464 | tf_op jit(solution)/shard_map/ppermute | solution.py:34
  888.7 50.2 %collective-permute-start.45 = (f32[1024,512]{1,0:T(8,128)}, f32[1024,512]{1,0:T(8,128)}, u32[]{:S(2)}, u32[]{:S(2)}) collective-permute-start(f32[1024,512]{1,0:T(8,128)} %add_add_fusion.5), channel_id=1, source_target_pairs={{0,8},{1,9},{2,10},{3,11},{4,12},{5,13},{6,14},{7,15},{8,24},{9,25... | collective-permute-start | bytes 6291464 | tf_op jit(solution)/shard_map/ppermute | solution.py:34
  893.3 50.0 %collective-permute-start.46 = (f32[1024,512]{1,0:T(8,128)}, f32[1024,512]{1,0:T(8,128)}, u32[]{:S(2)}, u32[]{:S(2)}) collective-permute-start(f32[1024,512]{1,0:T(8,128)} %get-tuple-element.154), channel_id=1, source_target_pairs={{0,1},{1,0},{2,3},{3,2},{4,5},{5,4},{6,7},{7,6},{8,9},{9,8},{10,11... | collective-permute-start | bytes 6291464 | tf_op jit(solution)/shard_map/ppermute | solution.py:34
  893.4 90.4 %collective-permute-start.52 = (f32[1024,512]{1,0:T(8,128)S(1)}, f32[1024,512]{1,0:T(8,128)}, u32[]{:S(2)}, u32[]{:S(2)}) collective-permute-start(f32[1024,512]{1,0:T(8,128)S(1)} %add_add_fusion.3), channel_id=1, source_target_pairs={{0,8},{1,9},{2,10},{3,11},{4,12},{5,13},{6,14},{7,15},{8,24},{9,25... | collective-permute-start | bytes 6291464 | tf_op jit(solution)/shard_map/ppermute | solution.py:34
  898.7 89.6 %collective-permute-start.53 = (f32[512,1024]{1,0:T(8,128)}, f32[512,1024]{1,0:T(8,128)}, u32[]{:S(2)}, u32[]{:S(2)}) collective-permute-start(f32[512,1024]{1,0:T(8,128)} %get-tuple-element.162), channel_id=1, source_target_pairs={{0,1},{1,0},{2,3},{3,2},{4,5},{5,4},{6,7},{7,6},{8,9},{9,8},{10,11... | collective-permute-start | bytes 6291464 | tf_op jit(solution)/shard_map/ppermute | solution.py:34
  898.9 128.1 %collective-permute-start.59 = (f32[512,1024]{1,0:T(8,128)}, f32[512,1024]{1,0:T(8,128)}, u32[]{:S(2)}, u32[]{:S(2)}) collective-permute-start(f32[512,1024]{1,0:T(8,128)} %add_add_fusion.1), channel_id=1, source_target_pairs={{0,8},{1,9},{2,10},{3,11},{4,12},{5,13},{6,14},{7,15},{8,24},{9,25... | collective-permute-start | bytes 6291464 | tf_op jit(solution)/shard_map/ppermute | solution.py:34
  (61 other events, 1914.5 us)
Sparse Core Ops, SparseCore 0:
  624.7 230.8 all-reduce.2
  884.3 239.2 all-reduce.4

commit v2 on v1

--- a/solution.py
+++ b/solution.py
@@ -138,22 +138,25 @@
         pairs = ((dwg_v, dwg_out), (dwu_v, dwu_out), (dwd_v, dwd_out))
         return [pltpu.make_async_copy(src, dst, dw_sem.at[i]) for i, (src, dst) in enumerate(pairs)]
 
-    for copy in weight_copies()[:2]:
+    first = row_copies(0, 0)
+    loads = weight_copies()
+    for copy in (first[0], loads[0], loads[1], first[1], first[2], loads[2], *row_copies(1, 1)):
         copy.start()
-    for t in range(n_blk):
-        for copy in row_copies(t, t):
-            copy.start()
-        if t == 0:
-            weight_copies()[2].start()
     for t in range(n_blk):
         pos_v[t:t + 1, :] = pos[t][slot_j:slot_j + 1, :]
     slot = lax.broadcasted_iota(jnp.int32, (capacity, tok_count), 0).astype(F32)
-    for copy in weight_copies():
+    for copy in loads[:2]:
         copy.wait()
 
     def block_body(t, carry):
-        for copy in row_copies(t, 0):
-            copy.wait()
+        for later in range(2, n_blk):
+            @pl.when(t == later - 2)
+            def _():
+                for copy in row_copies(later, later):
+                    copy.start()
+
+        copy_x, copy_dy, copy_w = row_copies(t, 0)
+        copy_x.wait()
         rows = pl.ds(pl.multiple_of(t * capacity, 64), capacity)
         x = xs_v[rows, :]
         g = dot_nn(x, wg_v[...])
@@ -162,6 +165,13 @@
         act = g * sig
         h = (act * u).astype(BF16)
         h_v[rows, :] = h
+
+        @pl.when(t == 0)
+        def _():
+            loads[2].wait()
+
+        copy_dy.wait()
+        copy_w.wait()
         o = dot_nn(h, wd_v[...]).astype(BF16)
         o_v[rows, :] = o
         d_raw = dr_v[rows, :].astype(F32)
@@ -189,7 +199,8 @@
         return carry
 
     lax.fori_loop(0, xs_v.shape[1] // 256, gate_body, 0)
-    for copy in dw_copies()[:2]:
+    stores = dw_copies()
+    for copy in stores[:2]:
         copy.start()
 
     def down_body(m, carry):
@@ -198,11 +209,11 @@
         return carry
 
     lax.fori_loop(0, h_v.shape[1] // 256, down_body, 0)
-    dw_copies()[2].start()
+    stores[2].start()
     for t in range(n_blk):
         for copy in out_copies(t):
             copy.wait()
-    for copy in dw_copies():
+    for copy in stores:
         copy.wait()
 
 
@@ -349,7 +360,7 @@
         dys_all = (dy_loc, dy_x, dy_y, dy_d)
 
         mine = [(wg_loc[0], wu_loc[0], wd_loc[0])]
-        for _ in range(3):
+        for _ in range(1, 4):
             mine.append(tuple(send(w, PERM_Z) for w in mine[-1]))
         other = [tuple(send(w, PERM_C) for w in ws) for ws in mine]
 
@@ -368,7 +379,9 @@
 
         gather, expert_call, combine_call = make_calls(capacity, tok_count, model_dim, ff_dim, n_exp)
         metas = (meta, meta_x, meta_y, meta_d)
-        gathered = [gather(eid, x, dy, m) for x, dy, m in zip(xs_all, dys_all, metas)]
+        gathered = []
+        for t in range(4):
+            gathered.append(gather(eid, xs_all[t], dys_all[t], metas[t]))
         xs, dr, ws, pos, gate = zip(*gathered)
 
         o_j, dx_j, a_j = [None] * 8, [None] * 8, [None] * 8

time: 1140 us -> 1130 us (level)
  no operation moved by 1% of the time
where the time goes in v2:
time: 1130 us
  waiting for transfers between devices  640 us (57%)
  Pallas kernels  326 us (29%)
  other arithmetic  77.5 us (7%)
  starting transfers between devices  54.3 us (5%)
  between operations  16.6 us (1%)
  local copies, waits for them, and re-layouts  13.7 us (1%)
    ppermute x60, waiting for transfers between devices, send(): return lax.ppermute(value, 'ep', perm)  364 us
    psum x1, waiting for transfers between devices, block_body(): stat = lax.psum(stat, 'ep')  184 us
    pallas_call x8, Pallas kernels, experts(): pl.pallas_call(functools.partial(expert_kernel, j, capacity), out_shape=(...  174 us
    psum x1, waiting for transfers between devices, block_body(): dw_router = lax.psum(dwr_t, 'ep').T  92.4 us
    pallas_call x4, Pallas kernels, combine(): pl.pallas_call(functools.partial(combine_kernel, capacity), grid=(tok_cou...  80.8 us
    pallas_call x4, Pallas kernels, gather(): pl.pallas_call(functools.partial(gather_kernel, capacity), grid=(4,), out...  62.2 us
    ppermute x60, starting transfers between devices, send(): return lax.ppermute(value, 'ep', perm)  54.2 us
    add x6, other arithmetic, block_body(): total = [part + came for part, came in zip(total, travel)]  24.4 us
  transfers between devices with their start and end apart: 62, of which 23 were waited for; matrix products, arithmetic and copies ran while one was open for 8% of the time, Pallas kernels for 29%

profile of v2, /device:TPU:0, one launch (start us, length us, event | category | flops | bytes accessed | tf_op | source)
XLA Modules:
  0.0 1128.6 jit_solution(7749864312343363053)
XLA Ops:
  13.4 22.3 %collective-permute-done.12.refs_16_ = bf16[1024,512]{1,0:T(8,128)(2,1)} collective-permute-done((bf16[1024,512]{1,0:T(8,128)(2,1)}, bf16[1024,512]{1,0:T(8,128)(2,1)}, u32[]{:S(2)}, u32[]{:S(2)}) %collective-permute-start.12) | collective-permute-done | bytes 1048608 | tf_op jit(solution)/shard_map/ppermute | solution.py:34
  44.9 4.6 collective-permute-done.8.meta_ref
  51.0 7.0 collective-permute-done.13.refs_17_
  62.3 18.2 %collective-permute-done.14.refs_18_ = bf16[512,1024]{1,0:T(8,128)(2,1)S(1)} collective-permute-done((bf16[512,1024]{1,0:T(8,128)(2,1)}, bf16[512,1024]{1,0:T(8,128)(2,1)S(1)}, u32[]{:S(2)}, u32[]{:S(2)}) %collective-permute-start.14) | collective-permute-done | bytes 1048608 | tf_op jit(solution)/shard_map/ppermute | solution.py:34
  82.3 20.8 %collective-permute-done.18.refs_16_ = bf16[1024,512]{1,0:T(8,128)(2,1)} collective-permute-done((bf16[1024,512]{1,0:T(8,128)(2,1)}, bf16[1024,512]{1,0:T(8,128)(2,1)}, u32[]{:S(2)}, u32[]{:S(2)}) %collective-permute-start.18) | collective-permute-done | bytes 1048608 | tf_op jit(solution)/shard_map/ppermute | solution.py:34
  104.9 19.8 %collective-permute-done.19.refs_17_ = bf16[1024,512]{1,0:T(8,128)(2,1)} collective-permute-done((bf16[1024,512]{1,0:T(8,128)(2,1)S(1)}, bf16[1024,512]{1,0:T(8,128)(2,1)}, u32[]{:S(2)}, u32[]{:S(2)}) %collective-permute-start.19) | collective-permute-done | bytes 1048608 | tf_op jit(solution)/shard_map/ppermute | solution.py:34
  129.2 20.8 %collective-permute-done.20.refs_18_ = bf16[512,1024]{1,0:T(8,128)(2,1)} collective-permute-done((bf16[512,1024]{1,0:T(8,128)(2,1)S(1)}, bf16[512,1024]{1,0:T(8,128)(2,1)}, u32[]{:S(2)}, u32[]{:S(2)}) %collective-permute-start.20) | collective-permute-done | bytes 1048608 | tf_op jit(solution)/shard_map/ppermute | solution.py:34
  157.0 15.9 %gather.13 = (bf16[2560,1024]{1,0:T(8,128)(2,1)}, bf16[2560,1024]{1,0:T(8,128)(2,1)}, f32[2560,128]{1,0:T(8,128)}, f32[8,1024]{1,0:T(8,128)}, f32[8,1024]{1,0:T(8,128)}) custom-call(s32[8]{0:T(128)} %reshape.195.eid_ref, bf16[1024,1024]{1,0:T(8,128)(2,1)} %x_ref.5, bf16[1024,1024]{1,0:T(8,128)(2,1)} %dy_ref.1, f32[64,1024]{1,0:T(8,128)} %get-tuple-element.88.meta_ref), custom_call_target="tpu_custom_call" | custom-call | flops 10737418240 | bytes 16000000 | tf_op jit(solution)/shard_map/gather/pallas_call | solution.py:282
  173.0 15.5 %gather.15 = (bf16[2560,1024]{1,0:T(8,128)(2,1)}, bf16[2560,1024]{1,0:T(8,128)(2,1)}, f32[2560,128]{1,0:T(8,128)}, f32[8,1024]{1,0:T(8,128)}, f32[8,1024]{1,0:T(8,128)}) custom-call(s32[8]{0:T(128)} %reshape.195.eid_ref, bf16[1024,1024]{1,0:T(8,128)(2,1)} %collective-permute-done.3.x_ref, bf16[1024,1024]{1,0:T(8,128)(2,1)} %collective-permute-done.4.dy_ref, ...), custom_call_target="tpu_custom_call" | custom-call | flops 10737418240 | bytes 16000000 | tf_op jit(solution)/shard_map/gather/pallas_call | solution.py:282
  188.6 11.2 collective-permute-done.25.refs_17_
  199.7 19.9 %collective-permute-done.26.refs_18_ = bf16[512,1024]{1,0:T(8,128)(2,1)} collective-permute-done((bf16[512,1024]{1,0:T(8,128)(2,1)}, bf16[512,1024]{1,0:T(8,128)(2,1)}, u32[]{:S(2)}, u32[]{:S(2)}) %collective-permute-start.26) | collective-permute-done | bytes 1048608 | tf_op jit(solution)/shard_map/ppermute | solution.py:34
  219.6 15.4 %gather.14 = (bf16[2560,1024]{1,0:T(8,128)(2,1)}, bf16[2560,1024]{1,0:T(8,128)(2,1)}, f32[2560,128]{1,0:T(8,128)}, f32[8,1024]{1,0:T(8,128)}, f32[8,1024]{1,0:T(8,128)}) custom-call(s32[8]{0:T(128)} %reshape.195.eid_ref, bf16[1024,1024]{1,0:T(8,128)(2,1)} %collective-permute-done.x_ref, bf16[1024,1024]{1,0:T(8,128)(2,1)} %collective-permute-done.1.dy_ref, ...), custom_call_target="tpu_custom_call" | custom-call | flops 10737418240 | bytes 16000000 | tf_op jit(solution)/shard_map/gather/pallas_call | solution.py:282
  235.7 15.4 %gather.16 = (bf16[2560,1024]{1,0:T(8,128)(2,1)}, bf16[2560,1024]{1,0:T(8,128)(2,1)}, f32[2560,128]{1,0:T(8,128)}, f32[8,1024]{1,0:T(8,128)}, f32[8,1024]{1,0:T(8,128)}) custom-call(s32[8]{0:T(128)} %reshape.195.eid_ref, bf16[1024,1024]{1,0:T(8,128)(2,1)} %collective-permute-done.6.x_ref, bf16[1024,1024]{1,0:T(8,128)(2,1)} %collective-permute-done.7.dy_ref, ...), custom_call_target="tpu_custom_call" | custom-call | flops 10737418240 | bytes 16000000 | tf_op jit(solution)/shard_map/gather/pallas_call | solution.py:282
  252.1 21.9 %experts.15 = (bf16[4,320,1024]{2,1,0:T(8,128)(2,1)}, bf16[4,320,1024]{2,1,0:T(8,128)(2,1)}, f32[4,1024]{1,0:T(4,128)}, f32[1024,512]{1,0:T(8,128)}, f32[1024,512]{1,0:T(8,128)}, /*index=5*/f32[512,1024]{1,0:T(8,128)}) custom-call(bf16[2560,1024]{1,0:T(8,128)(2,1)} %get-tuple-element.89.refs_0_, bf16[2560,1024]{1,0:T(8,128)(2,1)} %get-tuple-element.90.refs_1_, ...), custom_call_target="tpu_custom_call" | custom-call | flops 12079595520 | bytes 20000000 | tf_op jit(solution)/shard_map/experts/pallas_call | solution.py:295
  275.5 21.7 %experts.14 = (bf16[4,320,1024]{2,1,0:T(8,128)(2,1)}, bf16[4,320,1024]{2,1,0:T(8,128)(2,1)}, f32[4,1024]{1,0:T(4,128)}, f32[1024,512]{1,0:T(8,128)}, f32[1024,512]{1,0:T(8,128)}, /*index=5*/f32[512,1024]{1,0:T(8,128)}) custom-call(bf16[2560,1024]{1,0:T(8,128)(2,1)} %get-tuple-element.89.refs_0_, bf16[2560,1024]{1,0:T(8,128)(2,1)} %get-tuple-element.90.refs_1_, ...), custom_call_target="tpu_custom_call" | custom-call | flops 12079595520 | bytes 20000000 | tf_op jit(solution)/shard_map/experts/pallas_call | solution.py:295
  298.1 21.6 %experts.8 = (bf16[4,320,1024]{2,1,0:T(8,128)(2,1)}, bf16[4,320,1024]{2,1,0:T(8,128)(2,1)}, f32[4,1024]{1,0:T(4,128)}, f32[1024,512]{1,0:T(8,128)}, f32[1024,512]{1,0:T(8,128)}, /*index=5*/f32[512,1024]{1,0:T(8,128)}) custom-call(bf16[2560,1024]{1,0:T(8,128)(2,1)} %get-tuple-element.89.refs_0_, bf16[2560,1024]{1,0:T(8,128)(2,1)} %get-tuple-element.90.refs_1_, ...), custom_call_target="tpu_custom_call" | custom-call | flops 12079595520 | bytes 20000000 | tf_op jit(solution)/shard_map/experts/pallas_call | solution.py:295
  321.0 21.7 %experts.13 = (bf16[4,320,1024]{2,1,0:T(8,128)(2,1)}, bf16[4,320,1024]{2,1,0:T(8,128)(2,1)}, f32[4,1024]{1,0:T(4,128)}, f32[1024,512]{1,0:T(8,128)}, f32[1024,512]{1,0:T(8,128)}, /*index=5*/f32[512,1024]{1,0:T(8,128)}) custom-call(bf16[2560,1024]{1,0:T(8,128)(2,1)} %get-tuple-element.89.refs_0_, bf16[2560,1024]{1,0:T(8,128)(2,1)} %get-tuple-element.90.refs_1_, ...), custom_call_target="tpu_custom_call" | custom-call | flops 12079595520 | bytes 20000000 | tf_op jit(solution)/shard_map/experts/pallas_call | solution.py:295
  343.6 21.9 %experts.12 = (bf16[4,320,1024]{2,1,0:T(8,128)(2,1)}, bf16[4,320,1024]{2,1,0:T(8,128)(2,1)}, f32[4,1024]{1,0:T(4,128)}, f32[1024,512]{1,0:T(8,128)}, f32[1024,512]{1,0:T(8,128)}, /*index=5*/f32[512,1024]{1,0:T(8,128)}) custom-call(bf16[2560,1024]{1,0:T(8,128)(2,1)} %get-tuple-element.89.refs_0_, bf16[2560,1024]{1,0:T(8,128)(2,1)} %get-tuple-element.90.refs_1_, ...), custom_call_target="tpu_custom_call" | custom-call | flops 12079595520 | bytes 20000000 | tf_op jit(solution)/shard_map/experts/pallas_call | solution.py:295
  365.5 21.7 %experts.10 = (bf16[4,320,1024]{2,1,0:T(8,128)(2,1)}, bf16[4,320,1024]{2,1,0:T(8,128)(2,1)}, f32[4,1024]{1,0:T(4,128)}, f32[1024,512]{1,0:T(8,128)}, f32[1024,512]{1,0:T(8,128)}, /*index=5*/f32[512,1024]{1,0:T(8,128)}) custom-call(bf16[2560,1024]{1,0:T(8,128)(2,1)} %get-tuple-element.89.refs_0_, bf16[2560,1024]{1,0:T(8,128)(2,1)} %get-tuple-element.90.refs_1_, ...), custom_call_target="tpu_custom_call" | custom-call | flops 12079595520 | bytes 20000000 | tf_op jit(solution)/shard_map/experts/pallas_call | solution.py:295
  388.2 21.7 %experts.11 = (bf16[4,320,1024]{2,1,0:T(8,128)(2,1)}, bf16[4,320,1024]{2,1,0:T(8,128)(2,1)}, f32[4,1024]{1,0:T(4,128)}, f32[1024,512]{1,0:T(8,128)}, f32[1024,512]{1,0:T(8,128)}, /*index=5*/f32[512,1024]{1,0:T(8,128)}) custom-call(bf16[2560,1024]{1,0:T(8,128)(2,1)} %get-tuple-element.89.refs_0_, bf16[2560,1024]{1,0:T(8,128)(2,1)} %get-tuple-element.90.refs_1_, ...), custom_call_target="tpu_custom_call" | custom-call | flops 12079595520 | bytes 20000000 | tf_op jit(solution)/shard_map/experts/pallas_call | solution.py:295
  411.6 22.1 %experts.9 = (bf16[4,320,1024]{2,1,0:T(8,128)(2,1)}, bf16[4,320,1024]{2,1,0:T(8,128)(2,1)}, f32[4,1024]{1,0:T(4,128)}, f32[1024,512]{1,0:T(8,128)}, f32[1024,512]{1,0:T(8,128)}, /*index=5*/f32[512,1024]{1,0:T(8,128)}) custom-call(bf16[2560,1024]{1,0:T(8,128)(2,1)} %get-tuple-element.89.refs_0_, bf16[2560,1024]{1,0:T(8,128)(2,1)} %get-tuple-element.90.refs_1_, ...), custom_call_target="tpu_custom_call" | custom-call | flops 12079595520 | bytes 20000000 | tf_op jit(solution)/shard_map/experts/pallas_call | solution.py:295
  453.2 20.2 %combine.7 = (f32[1024,1024]{1,0:T(8,128)}, f32[1024,1024]{1,0:T(8,128)}) custom-call(bf16[4,320,1024]{2,1,0:T(8,128)(2,1)} %get-tuple-element.105.refs_0_, bf16[4,320,1024]{2,1,0:T(8,128)(2,1)} %get-tuple-element.106.refs_1_, bf16[4,320,1024]{2,1,0:T(8,128)(2,1)} %get-tuple-element.107.refs_2_, bf16[4,320,1024]{2,1,0:T(8,128)(2,1)} %get-tuple-element.108.refs_3_, ...), custom_call_target="tpu_custom_call" | custom-call | flops 10737418240 | bytes 20000000 | tf_op jit(solution)/shard_map/combine/pallas_call | solution.py:316
  487.2 20.4 %combine.6 = (f32[1024,1024]{1,0:T(8,128)}, f32[1024,1024]{1,0:T(8,128)}) custom-call(bf16[4,320,1024]{2,1,0:T(8,128)(2,1)} %get-tuple-element.105.refs_0_, bf16[4,320,1024]{2,1,0:T(8,128)(2,1)} %get-tuple-element.106.refs_1_, bf16[4,320,1024]{2,1,0:T(8,128)(2,1)} %get-tuple-element.107.refs_2_, bf16[4,320,1024]{2,1,0:T(8,128)(2,1)} %get-tuple-element.108.refs_3_, ...), custom_call_target="tpu_custom_call" | custom-call | flops 10737418240 | bytes 20000000 | tf_op jit(solution)/shard_map/combine/pallas_call | solution.py:316
  508.2 3.6 add.370
  511.8 17.5 %collective-permute-done.43 = f32[1024,512]{1,0:T(8,128)} collective-permute-done((f32[1024,512]{1,0:T(8,128)}, f32[1024,512]{1,0:T(8,128)}, u32[]{:S(2)}, u32[]{:S(2)}) %collective-permute-start.43) | collective-permute-done | bytes 2097184 | tf_op jit(solution)/shard_map/ppermute | solution.py:34
  530.2 4.3 add_add_fusion.4
  534.4 39.8 %collective-permute-done.50 = f32[1024,512]{1,0:T(8,128)} collective-permute-done((f32[1024,512]{1,0:T(8,128)}, f32[1024,512]{1,0:T(8,128)}, u32[]{:S(2)}, u32[]{:S(2)}) %collective-permute-start.50) | collective-permute-done | bytes 2097184 | tf_op jit(solution)/shard_map/ppermute | solution.py:34
  575.1 20.1 %combine.5 = (f32[1024,1024]{1,0:T(8,128)}, f32[1024,1024]{1,0:T(8,128)}) custom-call(bf16[4,320,1024]{2,1,0:T(8,128)(2,1)} %get-tuple-element.105.refs_0_, bf16[4,320,1024]{2,1,0:T(8,128)(2,1)} %get-tuple-element.106.refs_1_, bf16[4,320,1024]{2,1,0:T(8,128)(2,1)} %get-tuple-element.107.refs_2_, bf16[4,320,1024]{2,1,0:T(8,128)(2,1)} %get-tuple-element.108.refs_3_, ...), custom_call_target="tpu_custom_call" | custom-call | flops 10737418240 | bytes 20000000 | tf_op jit(solution)/shard_map/combine/pallas_call | solution.py:316
  595.8 7.0 add.332
  603.3 5.3 add.335
  608.6 10.6 collective-permute-done.57
  621.0 4.4 add_add_fusion.2
  625.5 33.0 %collective-permute-done.33 = f32[1024,1024]{1,0:T(8,128)} collective-permute-done((f32[1024,1024]{1,0:T(8,128)}, f32[1024,1024]{1,0:T(8,128)}, u32[]{:S(2)}, u32[]{:S(2)}) %collective-permute-start.33) | collective-permute-done | bytes 4194336 | tf_op jit(solution)/shard_map/ppermute | solution.py:34
  659.2 4.2 add_add_fusion
  667.1 183.7 %all-reduce.3.cloned.1.call-done = f32[32,1024]{1,0:T(8,128)} async-done(((f32[32,1024]{1,0:T(8,128)}), f32[32,1024]{1,0:T(8,128)}) %all-reduce.3.cloned.1.call-update) | async-done | bytes 131088 | tf_op jit(solution)/shard_map/psum | solution.py:373
  854.1 20.1 %combine.4 = (f32[1024,1024]{1,0:T(8,128)}, f32[1024,1024]{1,0:T(8,128)}) custom-call(bf16[4,320,1024]{2,1,0:T(8,128)(2,1)} %get-tuple-element.105.refs_0_, bf16[4,320,1024]{2,1,0:T(8,128)(2,1)} %get-tuple-element.106.refs_1_, bf16[4,320,1024]{2,1,0:T(8,128)(2,1)} %get-tuple-element.107.refs_2_, bf16[4,320,1024]{2,1,0:T(8,128)(2,1)} %get-tuple-element.108.refs_3_, ...), custom_call_target="tpu_custom_call" | custom-call | flops 10737418240 | bytes 20000000 | tf_op jit(solution)/shard_map/combine/pallas_call | solution.py:316
  874.2 5.2 router.1
  879.5 4.4 add_add_fusion.5
  890.1 3.8 add_add_fusion.1
  895.0 6.2 add_convert_fusion.1
  901.2 6.6 add_convert_fusion
  907.8 26.4 %collective-permute-done.45 = f32[1024,512]{1,0:T(8,128)} collective-permute-done((f32[1024,512]{1,0:T(8,128)}, f32[1024,512]{1,0:T(8,128)}, u32[]{:S(2)}, u32[]{:S(2)}) %collective-permute-start.45) | collective-permute-done | bytes 2097184 | tf_op jit(solution)/shard_map/ppermute | solution.py:34
  934.1 4.4 add_bitcast_fusion.2
  938.6 40.5 %collective-permute-done.52 = f32[1024,512]{1,0:T(8,128)} collective-permute-done((f32[1024,512]{1,0:T(8,128)S(1)}, f32[1024,512]{1,0:T(8,128)}, u32[]{:S(2)}, u32[]{:S(2)}) %collective-permute-start.52) | collective-permute-done | bytes 2097184 | tf_op jit(solution)/shard_map/ppermute | solution.py:34
  979.1 4.4 add_bitcast_fusion.1
  983.5 38.7 %collective-permute-done.59 = f32[512,1024]{1,0:T(8,128)} collective-permute-done((f32[512,1024]{1,0:T(8,128)}, f32[512,1024]{1,0:T(8,128)}, u32[]{:S(2)}, u32[]{:S(2)}) %collective-permute-start.59) | collective-permute-done | bytes 2097184 | tf_op jit(solution)/shard_map/ppermute | solution.py:34
  1022.2 4.2 add_bitcast_fusion
  1026.4 92.4 %all-reduce.5.cloned.1.call-done = f32[1024,32]{0,1:T(8,128)} async-done(((f32[1024,32]{0,1:T(8,128)}), f32[1024,32]{0,1:T(8,128)}) %all-reduce.5.cloned.1.call-update) | async-done | bytes 131088 | tf_op jit(solution)/shard_map/psum | solution.py:425
  (237 shorter events, 99.2 us)
Async XLA Ops:
  7.2 843.6 %all-reduce.3.cloned.1.call-start = ((), (), s32[]{:S(2)}) async-start(), calls=%async_computation | async-start | bytes 262144 | tf_op jit(solution)/shard_map/psum | solution.py:373
  10.3 47.7 %collective-permute-start.13 = (bf16[1024,512]{1,0:T(8,128)(2,1)}, bf16[1024,512]{1,0:T(8,128)(2,1)S(1)}, u32[]{:S(2)}, u32[]{:S(2)}) collective-permute-start(bf16[1024,512]{1,0:T(8,128)(2,1)} %bitcast.33), channel_id=1, source_target_pairs={{0,8},{1,9},{2,10},{3,11},{4,12},{5,13},{6,14},{7,15},{8,24},{9,25... | collective-permute-start | bytes 3145736 | tf_op jit(solution)/shard_map/ppermute | solution.py:34
  12.9 67.6 %collective-permute-start.14 = (bf16[512,1024]{1,0:T(8,128)(2,1)}, bf16[512,1024]{1,0:T(8,128)(2,1)S(1)}, u32[]{:S(2)}, u32[]{:S(2)}) collective-permute-start(bf16[512,1024]{1,0:T(8,128)(2,1)} %bitcast.36), channel_id=1, source_target_pairs={{0,8},{1,9},{2,10},{3,11},{4,12},{5,13},{6,14},{7,15},{8,24},{9,25... | collective-permute-start | bytes 3145736 | tf_op jit(solution)/shard_map/ppermute | solution.py:34
  35.7 67.4 %collective-permute-start.18 = (bf16[1024,512]{1,0:T(8,128)(2,1)}, bf16[1024,512]{1,0:T(8,128)(2,1)}, u32[]{:S(2)}, u32[]{:S(2)}) collective-permute-start(bf16[1024,512]{1,0:T(8,128)(2,1)} %collective-permute-done.12.refs_16_), channel_id=1, source_target_pairs={{0,8},{1,9},{2,10},{3,11},{4,12},{5,13},{6,14},{7,15},{8,24},{9,25... | collective-permute-start | bytes 3145736 | tf_op jit(solution)/shard_map/ppermute | solution.py:34
  58.0 66.7 %collective-permute-start.19 = (bf16[1024,512]{1,0:T(8,128)(2,1)S(1)}, bf16[1024,512]{1,0:T(8,128)(2,1)}, u32[]{:S(2)}, u32[]{:S(2)}) collective-permute-start(bf16[1024,512]{1,0:T(8,128)(2,1)S(1)} %collective-permute-done.13.refs_17_), channel_id=1, source_target_pairs={{0,8},{1,9},{2,10},{3,11},{4,12},{5,13},{6,14},{7,15},{8,24},{9,25... | collective-permute-start | bytes 3145736 | tf_op jit(solution)/shard_map/ppermute | solution.py:34
  59.2 91.2 %collective-permute-start.4 = (bf16[1024,1024]{1,0:T(8,128)(2,1)}, bf16[1024,1024]{1,0:T(8,128)(2,1)}, u32[]{:S(2)}, u32[]{:S(2)}) collective-permute-start(bf16[1024,1024]{1,0:T(8,128)(2,1)} %dy_ref.1), channel_id=1, source_target_pairs={{0,4},{1,5},{2,6},{3,7},{4,0},{5,1},{6,2},{7,3},{8,12},{9,13},{10,... | collective-permute-start | bytes 6291464 | tf_op jit(solution)/shard_map/ppermute | solution.py:34
  60.8 93.2 %collective-permute-start.1 = (bf16[1024,1024]{1,0:T(8,128)(2,1)}, bf16[1024,1024]{1,0:T(8,128)(2,1)}, u32[]{:S(2)}, u32[]{:S(2)}) collective-permute-start(bf16[1024,1024]{1,0:T(8,128)(2,1)} %dy_ref.1), channel_id=1, source_target_pairs={{0,2},{1,3},{2,0},{3,1},{4,6},{5,7},{6,4},{7,5},{8,10},{9,11},{10,... | collective-permute-start | bytes 6291464 | tf_op jit(solution)/shard_map/ppermute | solution.py:34
  80.5 73.5 %collective-permute-start = (bf16[1024,1024]{1,0:T(8,128)(2,1)}, bf16[1024,1024]{1,0:T(8,128)(2,1)}, u32[]{:S(2)}, u32[]{:S(2)}) collective-permute-start(bf16[1024,1024]{1,0:T(8,128)(2,1)} %x_ref.5), channel_id=1, source_target_pairs={{0,2},{1,3},{2,0},{3,1},{4,6},{5,7},{6,4},{7,5},{8,10},{9,11},{10,... | collective-permute-start | bytes 6291464 | tf_op jit(solution)/shard_map/ppermute | solution.py:34
  103.1 52.5 %collective-permute-start.3 = (bf16[1024,1024]{1,0:T(8,128)(2,1)}, bf16[1024,1024]{1,0:T(8,128)(2,1)}, u32[]{:S(2)}, u32[]{:S(2)}) collective-permute-start(bf16[1024,1024]{1,0:T(8,128)(2,1)} %x_ref.5), channel_id=1, source_target_pairs={{0,4},{1,5},{2,6},{3,7},{4,0},{5,1},{6,2},{7,3},{8,12},{9,13},{10,... | collective-permute-start | bytes 6291464 | tf_op jit(solution)/shard_map/ppermute | solution.py:34
  150.0 38.4 %collective-permute-start.24 = (bf16[1024,512]{1,0:T(8,128)(2,1)}, bf16[1024,512]{1,0:T(8,128)(2,1)}, u32[]{:S(2)}, u32[]{:S(2)}) collective-permute-start(bf16[1024,512]{1,0:T(8,128)(2,1)} %collective-permute-done.18.refs_16_), channel_id=1, source_target_pairs={{0,8},{1,9},{2,10},{3,11},{4,12},{5,13},{6,14},{7,15},{8,24},{9,25... | collective-permute-start | bytes 3145736 | tf_op jit(solution)/shard_map/ppermute | solution.py:34
  150.5 49.3 %collective-permute-start.25 = (bf16[1024,512]{1,0:T(8,128)(2,1)}, bf16[1024,512]{1,0:T(8,128)(2,1)}, u32[]{:S(2)}, u32[]{:S(2)}) collective-permute-start(bf16[1024,512]{1,0:T(8,128)(2,1)} %collective-permute-done.19.refs_17_), channel_id=1, source_target_pairs={{0,8},{1,9},{2,10},{3,11},{4,12},{5,13},{6,14},{7,15},{8,24},{9,25... | collective-permute-start | bytes 3145736 | tf_op jit(solution)/shard_map/ppermute | solution.py:34
  154.0 65.7 %collective-permute-start.26 = (bf16[512,1024]{1,0:T(8,128)(2,1)}, bf16[512,1024]{1,0:T(8,128)(2,1)}, u32[]{:S(2)}, u32[]{:S(2)}) collective-permute-start(bf16[512,1024]{1,0:T(8,128)(2,1)} %collective-permute-done.20.refs_18_), channel_id=1, source_target_pairs={{0,8},{1,9},{2,10},{3,11},{4,12},{5,13},{6,14},{7,15},{8,24},{9,25... | collective-permute-start | bytes 3145736 | tf_op jit(solution)/shard_map/ppermute | solution.py:34
  154.0 81.1 %collective-permute-start.7 = (bf16[1024,1024]{1,0:T(8,128)(2,1)}, bf16[1024,1024]{1,0:T(8,128)(2,1)}, u32[]{:S(2)}, u32[]{:S(2)}) collective-permute-start(bf16[1024,1024]{1,0:T(8,128)(2,1)} %collective-permute-done.4.dy_ref), channel_id=1, source_target_pairs={{0,2},{1,3},{2,0},{3,1},{4,6},{5,7},{6,4},{7,5},{8,10},{9,11},{10,... | collective-permute-start | bytes 6291464 | tf_op jit(solution)/shard_map/ppermute | solution.py:34
  155.5 80.1 %collective-permute-start.6 = (bf16[1024,1024]{1,0:T(8,128)(2,1)}, bf16[1024,1024]{1,0:T(8,128)(2,1)}, u32[]{:S(2)}, u32[]{:S(2)}) collective-permute-start(bf16[1024,1024]{1,0:T(8,128)(2,1)} %collective-permute-done.x_ref), channel_id=1, source_target_pairs={{0,4},{1,5},{2,6},{3,7},{4,0},{5,1},{6,2},{7,3},{8,12},{9,13},{10,... | collective-permute-start | bytes 6291464 | tf_op jit(solution)/shard_map/ppermute | solution.py:34
  188.5 62.7 %collective-permute-start.27 = (bf16[1024,512]{1,0:T(8,128)(2,1)}, bf16[1024,512]{1,0:T(8,128)(2,1)}, u32[]{:S(2)}, u32[]{:S(2)}) collective-permute-start(bf16[1024,512]{1,0:T(8,128)(2,1)} %collective-permute-done.24.refs_16_), channel_id=1, source_target_pairs={{0,1},{1,0},{2,3},{3,2},{4,5},{5,4},{6,7},{7,6},{8,9},{9,8},{10,11... | collective-permute-start | bytes 3145736 | tf_op jit(solution)/shard_map/ppermute | solution.py:34
  199.7 51.8 %collective-permute-start.28 = (bf16[1024,512]{1,0:T(8,128)(2,1)}, bf16[1024,512]{1,0:T(8,128)(2,1)}, u32[]{:S(2)}, u32[]{:S(2)}) collective-permute-start(bf16[1024,512]{1,0:T(8,128)(2,1)} %collective-permute-done.25.refs_17_), channel_id=1, source_target_pairs={{0,1},{1,0},{2,3},{3,2},{4,5},{5,4},{6,7},{7,6},{8,9},{9,8},{10,11... | collective-permute-start | bytes 3145736 | tf_op jit(solution)/shard_map/ppermute | solution.py:34
  235.1 174.9 %collective-permute-start.9 = (bf16[1024,512]{1,0:T(8,128)(2,1)S(1)}, bf16[1024,512]{1,0:T(8,128)(2,1)}, u32[]{:S(2)}, u32[]{:S(2)}) collective-permute-start(bf16[1024,512]{1,0:T(8,128)(2,1)S(1)} %bitcast.32), channel_id=1, source_target_pairs={{0,1},{1,0},{2,3},{3,2},{4,5},{5,4},{6,7},{7,6},{8,9},{9,8},{10,11... | collective-permute-start | bytes 3145736 | tf_op jit(solution)/shard_map/ppermute | solution.py:34
  235.6 174.7 %collective-permute-start.10 = (bf16[1024,512]{1,0:T(8,128)(2,1)S(1)}, bf16[1024,512]{1,0:T(8,128)(2,1)}, u32[]{:S(2)}, u32[]{:S(2)}) collective-permute-start(bf16[1024,512]{1,0:T(8,128)(2,1)S(1)} %bitcast.35), channel_id=1, source_target_pairs={{0,1},{1,0},{2,3},{3,2},{4,5},{5,4},{6,7},{7,6},{8,9},{9,8},{10,11... | collective-permute-start | bytes 3145736 | tf_op jit(solution)/shard_map/ppermute | solution.py:34
  251.1 68.6 %collective-permute-start.21 = (bf16[1024,512]{1,0:T(8,128)(2,1)}, bf16[1024,512]{1,0:T(8,128)(2,1)S(1)}, u32[]{:S(2)}, u32[]{:S(2)}) collective-permute-start(bf16[1024,512]{1,0:T(8,128)(2,1)} %collective-permute-done.18.refs_16_), channel_id=1, source_target_pairs={{0,1},{1,0},{2,3},{3,2},{4,5},{5,4},{6,7},{7,6},{8,9},{9,8},{10,11... | collective-permute-start | bytes 3145736 | tf_op jit(solution)/shard_map/ppermute | solution.py:34
  251.6 68.3 %collective-permute-start.22 = (bf16[1024,512]{1,0:T(8,128)(2,1)}, bf16[1024,512]{1,0:T(8,128)(2,1)S(1)}, u32[]{:S(2)}, u32[]{:S(2)}) collective-permute-start(bf16[1024,512]{1,0:T(8,128)(2,1)} %collective-permute-done.19.refs_17_), channel_id=1, source_target_pairs={{0,1},{1,0},{2,3},{3,2},{4,5},{5,4},{6,7},{7,6},{8,9},{9,8},{10,11... | collective-permute-start | bytes 3145736 | tf_op jit(solution)/shard_map/ppermute | solution.py:34
  251.7 68.7 %collective-permute-start.23 = (bf16[512,1024]{1,0:T(8,128)(2,1)}, bf16[512,1024]{1,0:T(8,128)(2,1)}, u32[]{:S(2)}, u32[]{:S(2)}) collective-permute-start(bf16[512,1024]{1,0:T(8,128)(2,1)} %collective-permute-done.20.refs_18_), channel_id=1, source_target_pairs={{0,1},{1,0},{2,3},{3,2},{4,5},{5,4},{6,7},{7,6},{8,9},{9,8},{10,11... | collective-permute-start | bytes 3145736 | tf_op jit(solution)/shard_map/ppermute | solution.py:34
  319.7 67.5 %collective-permute-start.15 = (bf16[1024,512]{1,0:T(8,128)(2,1)}, bf16[1024,512]{1,0:T(8,128)(2,1)S(1)}, u32[]{:S(2)}, u32[]{:S(2)}) collective-permute-start(bf16[1024,512]{1,0:T(8,128)(2,1)} %collective-permute-done.12.refs_16_), channel_id=1, source_target_pairs={{0,1},{1,0},{2,3},{3,2},{4,5},{5,4},{6,7},{7,6},{8,9},{9,8},{10,11... | collective-permute-start | bytes 3145736 | tf_op jit(solution)/shard_map/ppermute | solution.py:34
  319.9 67.7 %collective-permute-start.16 = (bf16[1024,512]{1,0:T(8,128)(2,1)S(1)}, bf16[1024,512]{1,0:T(8,128)(2,1)}, u32[]{:S(2)}, u32[]{:S(2)}) collective-permute-start(bf16[1024,512]{1,0:T(8,128)(2,1)S(1)} %copy-done.25), channel_id=1, source_target_pairs={{0,1},{1,0},{2,3},{3,2},{4,5},{5,4},{6,7},{7,6},{8,9},{9,8},{10,11... | collective-permute-start | bytes 3145736 | tf_op jit(solution)/shard_map/ppermute | solution.py:34
  320.4 67.5 %collective-permute-start.17 = (bf16[512,1024]{1,0:T(8,128)(2,1)S(1)}, bf16[512,1024]{1,0:T(8,128)(2,1)}, u32[]{:S(2)}, u32[]{:S(2)}) collective-permute-start(bf16[512,1024]{1,0:T(8,128)(2,1)S(1)} %collective-permute-done.14.refs_18_), channel_id=1, source_target_pairs={{0,1},{1,0},{2,3},{3,2},{4,5},{5,4},{6,7},{7,6},{8,9},{9,8},{10,11... | collective-permute-start | bytes 3145736 | tf_op jit(solution)/shard_map/ppermute | solution.py:34
  387.6 59.9 %collective-permute-start.40 = (f32[1024,512]{1,0:T(8,128)}, f32[1024,512]{1,0:T(8,128)}, u32[]{:S(2)}, u32[]{:S(2)}) collective-permute-start(f32[1024,512]{1,0:T(8,128)} %get-tuple-element.148), channel_id=1, source_target_pairs={{0,1},{1,0},{2,3},{3,2},{4,5},{5,4},{6,7},{7,6},{8,9},{9,8},{10,11... | collective-permute-start | bytes 6291464 | tf_op jit(solution)/shard_map/ppermute | solution.py:34
  387.9 60.2 %collective-permute-start.47 = (f32[1024,512]{1,0:T(8,128)}, f32[1024,512]{1,0:T(8,128)}, u32[]{:S(2)}, u32[]{:S(2)}) collective-permute-start(f32[1024,512]{1,0:T(8,128)} %get-tuple-element.156), channel_id=1, source_target_pairs={{0,1},{1,0},{2,3},{3,2},{4,5},{5,4},{6,7},{7,6},{8,9},{9,8},{10,11... | collective-permute-start | bytes 6291464 | tf_op jit(solution)/shard_map/ppermute | solution.py:34
  410.0 38.2 %collective-permute-start.54 = (f32[512,1024]{1,0:T(8,128)}, f32[512,1024]{1,0:T(8,128)S(1)}, u32[]{:S(2)}, u32[]{:S(2)}) collective-permute-start(f32[512,1024]{1,0:T(8,128)} %get-tuple-element.164), channel_id=1, source_target_pairs={{0,1},{1,0},{2,3},{3,2},{4,5},{5,4},{6,7},{7,6},{8,9},{9,8},{10,11... | collective-permute-start | bytes 6291464 | tf_op jit(solution)/shard_map/ppermute | solution.py:34
  410.4 38.2 %collective-permute-start.41 = (f32[1024,512]{1,0:T(8,128)}, f32[1024,512]{1,0:T(8,128)}, u32[]{:S(2)}, u32[]{:S(2)}) collective-permute-start(f32[1024,512]{1,0:T(8,128)} %get-tuple-element.150), channel_id=1, source_target_pairs={{0,1},{1,0},{2,3},{3,2},{4,5},{5,4},{6,7},{7,6},{8,9},{9,8},{10,11... | collective-permute-start | bytes 6291464 | tf_op jit(solution)/shard_map/ppermute | solution.py:34
  448.6 35.2 %collective-permute-start.56 = (f32[512,1024]{1,0:T(8,128)}, f32[512,1024]{1,0:T(8,128)}, u32[]{:S(2)}, u32[]{:S(2)}) collective-permute-start(f32[512,1024]{1,0:T(8,128)} %get-tuple-element.168), channel_id=1, source_target_pairs={{0,1},{1,0},{2,3},{3,2},{4,5},{5,4},{6,7},{7,6},{8,9},{9,8},{10,11... | collective-permute-start | bytes 6291464 | tf_op jit(solution)/shard_map/ppermute | solution.py:34
  451.9 55.7 %collective-permute-start.39 = (f32[1024,512]{1,0:T(8,128)}, f32[1024,512]{1,0:T(8,128)}, u32[]{:S(2)}, u32[]{:S(2)}) collective-permute-start(f32[1024,512]{1,0:T(8,128)} %get-tuple-element.146), channel_id=1, source_target_pairs={{0,1},{1,0},{2,3},{3,2},{4,5},{5,4},{6,7},{7,6},{8,9},{9,8},{10,11... | collective-permute-start | bytes 6291464 | tf_op jit(solution)/shard_map/ppermute | solution.py:34
  473.5 121.7 %collective-permute-start.31 = (f32[1024,1024]{1,0:T(8,128)}, f32[1024,1024]{1,0:T(8,128)}, u32[]{:S(2)}, u32[]{:S(2)}) collective-permute-start(f32[1024,1024]{1,0:T(8,128)} %get-tuple-element.128), channel_id=1, source_target_pairs={{0,2},{1,3},{2,0},{3,1},{4,6},{5,7},{6,4},{7,5},{8,10},{9,11},{10,... | collective-permute-start | bytes 12582920 | tf_op jit(solution)/shard_map/ppermute | solution.py:34
  474.5 128.2 %collective-permute-start.34 = (f32[1024,1024]{1,0:T(8,128)}, f32[1024,1024]{1,0:T(8,128)}, u32[]{:S(2)}, u32[]{:S(2)}) collective-permute-start(f32[1024,1024]{1,0:T(8,128)} %get-tuple-element.133), channel_id=1, source_target_pairs={{0,4},{1,5},{2,6},{3,7},{4,0},{5,1},{6,2},{7,3},{8,12},{9,13},{10,... | collective-permute-start | bytes 12582920 | tf_op jit(solution)/shard_map/ppermute | solution.py:34
  479.6 49.7 %collective-permute-start.43 = (f32[1024,512]{1,0:T(8,128)}, f32[1024,512]{1,0:T(8,128)}, u32[]{:S(2)}, u32[]{:S(2)}) collective-permute-start(f32[1024,512]{1,0:T(8,128)} %add.356), channel_id=1, source_target_pairs={{0,8},{1,9},{2,10},{3,11},{4,12},{5,13},{6,14},{7,15},{8,24},{9,25... | collective-permute-start | bytes 6291464 | tf_op jit(solution)/shard_map/ppermute | solution.py:34
  483.8 90.5 %collective-permute-start.50 = (f32[1024,512]{1,0:T(8,128)}, f32[1024,512]{1,0:T(8,128)}, u32[]{:S(2)}, u32[]{:S(2)}) collective-permute-start(f32[1024,512]{1,0:T(8,128)} %add.363), channel_id=1, source_target_pairs={{0,8},{1,9},{2,10},{3,11},{4,12},{5,13},{6,14},{7,15},{8,24},{9,25... | collective-permute-start | bytes 6291464 | tf_op jit(solution)/shard_map/ppermute | solution.py:34
  507.6 150.8 %collective-permute-start.33 = (f32[1024,1024]{1,0:T(8,128)}, f32[1024,1024]{1,0:T(8,128)}, u32[]{:S(2)}, u32[]{:S(2)}) collective-permute-start(f32[1024,1024]{1,0:T(8,128)} %get-tuple-element.131), channel_id=1, source_target_pairs={{0,4},{1,5},{2,6},{3,7},{4,0},{5,1},{6,2},{7,3},{8,12},{9,13},{10,... | collective-permute-start | bytes 12582920 | tf_op jit(solution)/shard_map/ppermute | solution.py:34
  529.3 89.9 %collective-permute-start.57 = (f32[512,1024]{1,0:T(8,128)}, f32[512,1024]{1,0:T(8,128)}, u32[]{:S(2)}, u32[]{:S(2)}) collective-permute-start(f32[512,1024]{1,0:T(8,128)} %add.370), channel_id=1, source_target_pairs={{0,8},{1,9},{2,10},{3,11},{4,12},{5,13},{6,14},{7,15},{8,24},{9,25... | collective-permute-start | bytes 6291464 | tf_op jit(solution)/shard_map/ppermute | solution.py:34
  574.3 90.5 %collective-permute-start.44 = (f32[1024,512]{1,0:T(8,128)}, f32[1024,512]{1,0:T(8,128)}, u32[]{:S(2)}, u32[]{:S(2)}) collective-permute-start(f32[1024,512]{1,0:T(8,128)} %add_add_fusion.4), channel_id=1, source_target_pairs={{0,8},{1,9},{2,10},{3,11},{4,12},{5,13},{6,14},{7,15},{8,24},{9,25... | collective-permute-start | bytes 6291464 | tf_op jit(solution)/shard_map/ppermute | solution.py:34
  595.2 293.4 %collective-permute-start.30 = (f32[1024,1024]{1,0:T(8,128)}, f32[1024,1024]{1,0:T(8,128)}, u32[]{:S(2)}, u32[]{:S(2)}) collective-permute-start(f32[1024,1024]{1,0:T(8,128)} %get-tuple-element.124), channel_id=1, source_target_pairs={{0,2},{1,3},{2,0},{3,1},{4,6},{5,7},{6,4},{7,5},{8,10},{9,11},{10,... | collective-permute-start | bytes 12582920 | tf_op jit(solution)/shard_map/ppermute | solution.py:34
  602.8 291.2 %collective-permute-start.32 = (f32[1024,1024]{1,0:T(8,128)}, f32[1024,1024]{1,0:T(8,128)}, u32[]{:S(2)}, u32[]{:S(2)}) collective-permute-start(f32[1024,1024]{1,0:T(8,128)} %add.332), channel_id=1, source_target_pairs={{0,4},{1,5},{2,6},{3,7},{4,0},{5,1},{6,2},{7,3},{8,12},{9,13},{10,... | collective-permute-start | bytes 12582920 | tf_op jit(solution)/shard_map/ppermute | solution.py:34
  619.2 274.9 %collective-permute-start.35 = (f32[1024,1024]{1,0:T(8,128)}, f32[1024,1024]{1,0:T(8,128)}, u32[]{:S(2)}, u32[]{:S(2)}) collective-permute-start(f32[1024,1024]{1,0:T(8,128)} %add.335), channel_id=1, source_target_pairs={{0,2},{1,3},{2,0},{3,1},{4,6},{5,7},{6,4},{7,5},{8,10},{9,11},{10,... | collective-permute-start | bytes 12582920 | tf_op jit(solution)/shard_map/ppermute | solution.py:34
  619.8 499.0 %all-reduce.5.cloned.1.call-start = ((), (), s32[]{:S(2)}) async-start(), calls=%async_computation.1 | async-start | bytes 262144 | tf_op jit(solution)/shard_map/psum | solution.py:425
  658.4 225.5 %collective-permute-start.51 = (f32[1024,512]{1,0:T(8,128)}, f32[1024,512]{1,0:T(8,128)}, u32[]{:S(2)}, u32[]{:S(2)}) collective-permute-start(f32[1024,512]{1,0:T(8,128)} %add_add_fusion.2), channel_id=1, source_target_pairs={{0,8},{1,9},{2,10},{3,11},{4,12},{5,13},{6,14},{7,15},{8,24},{9,25... | collective-permute-start | bytes 6291464 | tf_op jit(solution)/shard_map/ppermute | solution.py:34
  664.8 223.9 %collective-permute-start.58 = (f32[512,1024]{1,0:T(8,128)}, f32[512,1024]{1,0:T(8,128)}, u32[]{:S(2)}, u32[]{:S(2)}) collective-permute-start(f32[512,1024]{1,0:T(8,128)} %add_add_fusion), channel_id=1, source_target_pairs={{0,8},{1,9},{2,10},{3,11},{4,12},{5,13},{6,14},{7,15},{8,24},{9,25... | collective-permute-start | bytes 6291464 | tf_op jit(solution)/shard_map/ppermute | solution.py:34
  883.9 50.2 %collective-permute-start.45 = (f32[1024,512]{1,0:T(8,128)}, f32[1024,512]{1,0:T(8,128)}, u32[]{:S(2)}, u32[]{:S(2)}) collective-permute-start(f32[1024,512]{1,0:T(8,128)} %add_add_fusion.5), channel_id=1, source_target_pairs={{0,8},{1,9},{2,10},{3,11},{4,12},{5,13},{6,14},{7,15},{8,24},{9,25... | collective-permute-start | bytes 6291464 | tf_op jit(solution)/shard_map/ppermute | solution.py:34
  888.6 50.0 %collective-permute-start.46 = (f32[1024,512]{1,0:T(8,128)}, f32[1024,512]{1,0:T(8,128)}, u32[]{:S(2)}, u32[]{:S(2)}) collective-permute-start(f32[1024,512]{1,0:T(8,128)} %get-tuple-element.154), channel_id=1, source_target_pairs={{0,1},{1,0},{2,3},{3,2},{4,5},{5,4},{6,7},{7,6},{8,9},{9,8},{10,11... | collective-permute-start | bytes 6291464 | tf_op jit(solution)/shard_map/ppermute | solution.py:34
  888.6 90.4 %collective-permute-start.52 = (f32[1024,512]{1,0:T(8,128)S(1)}, f32[1024,512]{1,0:T(8,128)}, u32[]{:S(2)}, u32[]{:S(2)}) collective-permute-start(f32[1024,512]{1,0:T(8,128)S(1)} %add_add_fusion.3), channel_id=1, source_target_pairs={{0,8},{1,9},{2,10},{3,11},{4,12},{5,13},{6,14},{7,15},{8,24},{9,25... | collective-permute-start | bytes 6291464 | tf_op jit(solution)/shard_map/ppermute | solution.py:34
  894.0 89.6 %collective-permute-start.53 = (f32[512,1024]{1,0:T(8,128)}, f32[512,1024]{1,0:T(8,128)}, u32[]{:S(2)}, u32[]{:S(2)}) collective-permute-start(f32[512,1024]{1,0:T(8,128)} %get-tuple-element.162), channel_id=1, source_target_pairs={{0,1},{1,0},{2,3},{3,2},{4,5},{5,4},{6,7},{7,6},{8,9},{9,8},{10,11... | collective-permute-start | bytes 6291464 | tf_op jit(solution)/shard_map/ppermute | solution.py:34
  894.1 128.1 %collective-permute-start.59 = (f32[512,1024]{1,0:T(8,128)}, f32[512,1024]{1,0:T(8,128)}, u32[]{:S(2)}, u32[]{:S(2)}) collective-permute-start(f32[512,1024]{1,0:T(8,128)} %add_add_fusion.1), channel_id=1, source_target_pairs={{0,8},{1,9},{2,10},{3,11},{4,12},{5,13},{6,14},{7,15},{8,24},{9,25... | collective-permute-start | bytes 6291464 | tf_op jit(solution)/shard_map/ppermute | solution.py:34
  (61 other events, 1908.3 us)
Sparse Core Ops, SparseCore 0:
  619.9 230.8 all-reduce.2
  879.6 239.2 all-reduce.4
